TPU v7x, 256 devices: a whole 4x4x8 slice. The times are simulated.
256 devices in a mesh: group: 32 (over z, y_hi, core), helper: 8 (over y_lo, x).
Axes of the slice: x: 4, y: 4 (y_hi: 2, y_lo: 2; y = y_hi * 2 + y_lo), z: 8, core: 2. Of those that a mesh axis runs over, the one named last changes fastest.
Arguments:
- candidates: bfloat16 [32, 2048, 1024], P('group', 'helper'), may hold values from -6 to 6
- prefix_cache: bfloat16 [32, 2, 3072, 1024], P('group', None, 'helper'), may hold values from -6 to 6
- w_uvqk: bfloat16 [1024, 4096], replicated, may hold values from -0.1875 to 0.1875
- w_output: bfloat16 [1024, 1024], replicated, may hold values from -0.1875 to 0.1875
- norm_gain: float32 [1024], replicated, may hold values from 0.1 to 1.9
- owner: int32 [32], replicated, may hold values from 0 to 31, as said below
- counts: int32 [32], replicated, may hold values from 1024 to 2048, as said below
- prefix_len: int32 [32], replicated, may hold values from 96 to 3072, as said below
Outputs:
- update: bfloat16 [32, 2048, 1024], P('group', 'helper')
Inputs may be any that keep to these rules, and one draw needn't show every extreme that they name: owner[u] = (u + s) mod 32 for one shift s of the round. `counts`: multiples of 128; some user has exactly 2048. `prefix_len`: some user has exactly 3072.
All inputs are finite; a program needn't handle non-finite values.
Results may differ from a plain program's by a relative error of at most 0.012.
Values may be sent and summed in bfloat16 or wider, within the bound.
No kernel may reach another device: no remote copies, remote signals or barrier semaphores. Data moves between devices by JAX's collectives and lax.ppermute only.
A program may use at most 128 MiB of HBM per device.

v0:
```python
import functools

import jax
import jax.numpy as jnp
from jax import lax
from jax.experimental import pallas as pl
from jax.experimental.pallas import tpu as pltpu
from jax.sharding import PartitionSpec as P


HEADS = 8
FAR = 4


def silu(value):
    half = 0.5 * value
    return half + half * jnp.tanh(half)


def exchange(value):
    return lax.all_to_all(value, "helper", 0, 0, tiled=True)


def rotate(value, steps, count):
    if steps % count == 0:
        return value
    pairs = [(source, (source + steps) % count) for source in range(count)]
    return lax.ppermute(value, "group", pairs)


def near_move(steps, count, head):
    def move(tokens, cache, w_uvqk):
        moved = rotate(tokens, steps, count)
        split, w_query = prepare(cache, w_uvqk, head)
        return moved, split, w_query

    return move


def far_move(steps, count):
    def move(tokens, split):
        moved = rotate(tokens, steps, count)
        cache = exchange(split)
        return moved, cache

    return move


def route(offset, groups):
    signed = jnp.where(offset > groups // 2, offset - groups, offset)
    size = jnp.abs(signed)
    sign = jnp.where(signed < 0, -1, 1)
    most = groups // 2
    over = size > most - FAR
    near = jnp.where(over, size - most, size % FAR)
    far = jnp.where(over, most // FAR, size // FAR)
    return sign * near, sign * far


def limit(mebibytes):
    return pltpu.CompilerParams(vmem_limit_bytes=mebibytes << 20)


def prepare_kernel(cache_ref, w_uvqk_ref, split_ref, query_ref, sems):
    heads, _, _, head = split_ref.shape
    width = query_ref.shape[1]
    copies = [
        pltpu.make_async_copy(cache_ref.at[:, :, h * head : (h + 1) * head], split_ref.at[h], sems.at[h])
        for h in range(heads)
    ]
    copies.append(
        pltpu.make_async_copy(w_uvqk_ref.at[:, 2 * width : 3 * width], query_ref, sems.at[heads])
    )
    for copy in copies:
        copy.start()
    for copy in copies:
        copy.wait()


def prepare(cache, w_uvqk, head):
    two, length, width = cache.shape
    heads = width // head
    return pl.pallas_call(
        prepare_kernel,
        in_specs=[pl.BlockSpec(memory_space=pltpu.HBM), pl.BlockSpec(memory_space=pltpu.HBM)],
        out_specs=[pl.BlockSpec(memory_space=pltpu.VMEM), pl.BlockSpec(memory_space=pltpu.VMEM)],
        out_shape=[
            pltpu.VMEM((heads, two, length, head), cache.dtype),
            pltpu.VMEM((width, width), w_uvqk.dtype),
        ],
        scratch_shapes=[pltpu.SemaphoreType.DMA((heads + 1,))],
        compiler_params=limit(4),
        name="prepare",
    )(cache, w_uvqk)


def query_kernel(tokens_ref, w_ref, out_ref):
    heads, _, head = out_ref.shape
    tokens = tokens_ref[...]
    for h in range(0, heads, 2):
        cols = slice(h * head, (h + 2) * head)
        proj = jnp.dot(tokens, w_ref[:, cols], preferred_element_type=jnp.float32)
        proj = silu(proj).astype(jnp.bfloat16)
        out_ref[h] = proj[:, :head]
        out_ref[h + 1] = proj[:, head:]


def project_query(tokens, w_query, head):
    slots, width = tokens.shape
    heads = width // head
    return pl.pallas_call(
        query_kernel,
        out_shape=jax.ShapeDtypeStruct((heads, slots, head), jnp.bfloat16),
        cost_estimate=pl.CostEstimate(
            flops=2 * slots * width * width, bytes_accessed=2 * width * width, transcendentals=slots * width
        ),
        compiler_params=limit(8),
        name="project_query",
    )(tokens, w_query)


def own_kernel(scale, tokens_ref, query_ref, wu_ref, wv_ref, wk_ref, gate_ref, own_ref):
    per, _, head = query_ref.shape
    tokens = tokens_ref[...]
    gate_ref[...] = silu(jnp.dot(tokens, wu_ref[...], preferred_element_type=jnp.float32))
    own_v = silu(jnp.dot(tokens, wv_ref[...], preferred_element_type=jnp.float32)).astype(jnp.bfloat16)
    own_k = silu(jnp.dot(tokens, wk_ref[...], preferred_element_type=jnp.float32)).astype(jnp.bfloat16)
    for h in range(per):
        cols = slice(h * head, (h + 1) * head)
        query = query_ref[h].astype(jnp.float32)
        score = jnp.sum(query * own_k[:, cols].astype(jnp.float32), axis=-1, keepdims=True) * scale
        weight = silu(score).astype(jnp.bfloat16).astype(jnp.float32)
        own_ref[h] = weight * own_v[:, cols].astype(jnp.float32)


def project_own(tokens, query, w_uvqk, head):
    slots, width = tokens.shape
    heads = width // head
    cols = 2 * head
    per = cols // head
    steps = width // cols
    return pl.pallas_call(
        functools.partial(own_kernel, head ** (-0.5)),
        grid=(steps,),
        in_specs=[
            pl.BlockSpec((slots, width), lambda i: (0, 0)),
            pl.BlockSpec((per, slots, head), lambda i: (i, 0, 0)),
            pl.BlockSpec((width, cols), lambda i: (0, i)),
            pl.BlockSpec((width, cols), lambda i: (0, steps + i)),
            pl.BlockSpec((width, cols), lambda i: (0, 3 * steps + i)),
        ],
        out_specs=[
            pl.BlockSpec((slots, cols), lambda i: (0, i)),
            pl.BlockSpec((per, slots, head), lambda i: (i, 0, 0)),
        ],
        out_shape=[
            jax.ShapeDtypeStruct((slots, width), jnp.float32),
            jax.ShapeDtypeStruct((heads, slots, head), jnp.float32),
        ],
        cost_estimate=pl.CostEstimate(
            flops=6 * slots * width * width, bytes_accessed=6 * width * width, transcendentals=3 * slots * width
        ),
        compiler_params=limit(16),
        name="project_own",
    )(tokens, query, w_uvqk, w_uvqk, w_uvqk)


def attend_kernel(scale, rows, chunk, groups, meta_ref, query_ref, cache_ref, out_ref, keys_ref):
    blocks, slots, head = query_ref.shape
    shards, _, length, _ = cache_ref.shape
    per = rows // slots
    count = meta_ref[0]
    visible = meta_ref[1]
    live_blocks = jnp.minimum((count + rows - 1) // rows, blocks // per)

    def clear_keys(shard, carry):
        place = shard * length + lax.broadcasted_iota(jnp.int32, (length, head), 0)
        keys = cache_ref[shard, 0].astype(jnp.float32)
        keys_ref[shard] = jnp.where(place < visible, keys, 0.0).astype(jnp.bfloat16)
        return carry

    lax.fori_loop(0, shards, clear_keys, 0)

    def attend_to(used):
        span = used * length
        pieces = span // chunk

        def row_block(number, carry):
            first = number * per
            query = query_ref[pl.ds(first, per)].reshape(rows, head)
            query = (query.astype(jnp.float32) * (0.5 * scale)).astype(jnp.bfloat16)
            keys = keys_ref[:used].reshape(span, head)
            values = cache_ref[:used, 1].reshape(span, head)

            def scores(piece):
                part = keys[piece * chunk : (piece + 1) * chunk]
                return lax.dot_general(
                    query, part, (((1,), (1,)), ((), ())), preferred_element_type=jnp.float32
                )

            acc = jnp.zeros((rows, head), jnp.float32)
            ahead = scores(0)
            for piece in range(pieces):
                half = ahead.astype(jnp.bfloat16)
                if piece + 1 < pieces:
                    ahead = scores(piece + 1)
                weight = half + half * jnp.tanh(half)
                part = values[piece * chunk : (piece + 1) * chunk]
                acc = acc + jnp.dot(weight, part, preferred_element_type=jnp.float32)
            out_ref[pl.ds(first, per)] = acc.astype(jnp.bfloat16).reshape(per, slots, head)
            return carry

        lax.fori_loop(0, live_blocks, row_block, 0)

    below = 0
    for used in groups:
        within = visible > below * length
        if used < shards:
            within = jnp.logical_and(within, visible <= used * length)
        pl.when(within)(functools.partial(attend_to, used))
        below = used

    def dead_block(number, carry):
        out_ref[pl.ds(number * per, per)] = jnp.zeros((per, slots, head), jnp.bfloat16)
        return carry

    lax.fori_loop(live_blocks, blocks // per, dead_block, 0)


def attend(meta, query, cache):
    blocks, slots, head = query.shape
    shards, _, length, _ = cache.shape
    rows = 2 * slots
    chunk = length
    groups = (shards // 2, shards)
    flops = 4 * blocks * slots * shards * length * head
    return pl.pallas_call(
        functools.partial(attend_kernel, head ** (-0.5), rows, chunk, groups),
        grid_spec=pltpu.PrefetchScalarGridSpec(
            num_scalar_prefetch=1,
            grid=(1,),
            in_specs=[
                pl.BlockSpec(query.shape, lambda i, meta: (0, 0, 0)),
                pl.BlockSpec(cache.shape, lambda i, meta: (0, 0, 0, 0)),
            ],
            out_specs=pl.BlockSpec(query.shape, lambda i, meta: (0, 0, 0)),
            scratch_shapes=[pltpu.VMEM((shards, length, head), jnp.bfloat16)],
        ),
        out_shape=jax.ShapeDtypeStruct(query.shape, jnp.bfloat16),
        cost_estimate=pl.CostEstimate(
            flops=flops, bytes_accessed=cache.size * 2, transcendentals=blocks * slots * shards * length
        ),
        compiler_params=limit(24),
        name="attend",
    )(meta, query, cache)


def finish_kernel(pieces, meta_ref, mixed_ref, own_ref, gate_ref, gain_ref, w_ref, out_ref):
    heads, slots, head = mixed_ref.shape
    count = meta_ref[0]
    first = meta_ref[2] * slots
    width = heads * head
    rows = slots // pieces
    for piece in range(pieces):
        here = slice(piece * rows, (piece + 1) * rows)
        mixed = jnp.concatenate(
            [mixed_ref[h, here].astype(jnp.float32) + own_ref[h, here] for h in range(heads)], axis=1
        )
        centre = mixed - jnp.sum(mixed, axis=-1, keepdims=True) * (1.0 / width)
        spread = jnp.sum(centre * centre, axis=-1, keepdims=True) * (1.0 / width)
        normed = centre * lax.rsqrt(spread + 1e-05) * gain_ref[...] * gate_ref[here]
        result = jnp.dot(normed.astype(jnp.bfloat16), w_ref[...], preferred_element_type=jnp.float32)
        place = first + piece * rows + lax.broadcasted_iota(jnp.int32, result.shape, 0)
        out_ref[here] = jnp.where(place < count, result, 0.0).astype(jnp.bfloat16)


def finish(meta, mixed, own, gate, gain, w_output):
    slots, width = gate.shape
    return pl.pallas_call(
        functools.partial(finish_kernel, 2),
        grid_spec=pltpu.PrefetchScalarGridSpec(
            num_scalar_prefetch=1,
            grid=(1,),
            in_specs=[
                pl.BlockSpec(mixed.shape, lambda i, meta: (0, 0, 0)),
                pl.BlockSpec(own.shape, lambda i, meta: (0, 0, 0)),
                pl.BlockSpec(gate.shape, lambda i, meta: (0, 0)),
                pl.BlockSpec((1, width), lambda i, meta: (0, 0)),
                pl.BlockSpec(w_output.shape, lambda i, meta: (0, 0)),
            ],
            out_specs=pl.BlockSpec((slots, width), lambda i, meta: (0, 0)),
        ),
        out_shape=jax.ShapeDtypeStruct((slots, width), jnp.bfloat16),
        cost_estimate=pl.CostEstimate(
            flops=2 * slots * width * width, bytes_accessed=2 * width * width, transcendentals=slots
        ),
        compiler_params=limit(16),
        name="finish",
    )(meta, mixed, own, gate, gain.reshape(1, width), w_output)


def local(candidates, prefix_cache, w_uvqk, w_output, norm_gain, owner, counts, prefix_len):
    groups = lax.axis_size("group")
    group_here = lax.axis_index("group")
    helper_here = lax.axis_index("helper")
    offset = owner[0]
    width = candidates.shape[2]
    head = width // HEADS
    near, far = route(offset, groups)
    reach = groups // 2 // FAR
    nears = range(1 - FAR, FAR)
    fars = range(-reach, reach + 1)
    near_moves = [near_move(steps, groups, head) for steps in nears]
    far_moves = [far_move(FAR * steps, groups) for steps in fars]
    w_uvqk = pltpu.with_memory_space_constraint(w_uvqk, pltpu.HBM)
    prefix = pltpu.with_memory_space_constraint(prefix_cache[0], pltpu.HBM)
    tokens, split, w_query = lax.switch(near + FAR - 1, near_moves, candidates[0], prefix, w_uvqk)
    tokens, cache = lax.switch(far + reach, far_moves, tokens, split)
    user = (group_here - offset) % groups
    table = jnp.stack([counts, prefix_len, jnp.full_like(counts, helper_here)])
    places = lax.broadcasted_iota(jnp.int32, table.shape, 1)
    meta = jnp.sum(jnp.where(places == user, table, 0), axis=1)
    query = project_query(tokens, w_query, head)
    query_all = exchange(query)
    gate, own = project_own(tokens, query, w_uvqk, head)
    heads_out = attend(meta, query_all, cache)
    mixed = exchange(heads_out)
    return finish(meta, mixed, own, gate, norm_gain, w_output)[None]


def solution(mesh):
    in_specs = (
        P("group", "helper", None),
        P("group", None, "helper", None),
        P(),
        P(),
        P(),
        P(),
        P(),
        P(),
    )
    out_specs = P("group", "helper", None)
    return jax.shard_map(local, mesh=mesh, in_specs=in_specs, out_specs=out_specs, check_vma=False)
```

profile of v0, /device:TPU:32, one launch (start us, length us, event | category | flops | bytes accessed | tf_op | source)
XLA Modules:
  0.0 86.5 jit_solution(570922274464498651)
XLA Ops:
  2.0 5.4 %conditional.2 = (bf16[256,1024]{1,0:T(8,128)(2,1)}, bf16[8,2,384,128]{3,2,1,0:T(8,128)(2,1)}, bf16[1024,1024]{1,0:T(8,128)(2,1)S(1)}) conditional(s32[]{:T(128)} %clamp.7, (bf16[256,1024]{1,0:T(8,128)(2,1)}, bf16[2,384,1024]{2,1,0:T(8,128)(2,1)}, bf16[1024,4096]{1,0:T(8,128)(2,1)}) %tuple.96, ...), branch_computations={%region_1.2_spmd, %region_2.3_spmd, %region_3.4_spmd, %region_4.5_... | conditional | bytes 2097216 | solution.py:317
  2.0 1.9 %copy.18 = bf16[256,1024]{1,0:T(8,128)(2,1)} copy(bf16[256,1024]{1,0:T(8,128)(2,1)} %get-tuple-element.159) | data formatting | bytes 1048576 | tf_op jit(solution)/shard_map/cond
  3.9 3.5 %prepare.10 = (bf16[8,2,384,128]{3,2,1,0:T(8,128)(2,1)}, bf16[1024,1024]{1,0:T(8,128)(2,1)S(1)}) custom-call(bf16[2,384,1024]{2,1,0:T(8,128)(2,1)} %get-tuple-element.99.cache_ref, bf16[1024,4096]{1,0:T(8,128)(2,1)} %get-tuple-element.100.w_uvqk_ref), custom_call_target="tpu_custom_call" | custom-call | tf_op jit(solution)/shard_map/cond/branch_3_fun/prepare/pallas_call | solution.py:83
  7.4 34.0 %conditional.3 = (bf16[256,1024]{1,0:T(8,128)(2,1)}, bf16[8,2,384,128]{3,2,1,0:T(8,128)(2,1)}) conditional(s32[]{:T(128)} %clamp.6, (bf16[256,1024]{1,0:T(8,128)(2,1)}, bf16[8,2,384,128]{3,2,1,0:T(8,128)(2,1)}) %tuple.71, (bf16[256,1024]{1,0:T(8,128)(2,1)}, bf16[8,2,384,128]{3,2,1,0:T(8,128)(2,1)}) %tuple.71, ...), branch_computations={%region_8.9_spmd, %region_9.10_spmd, %region_10.11_spmd, %region_1... | conditional | bytes 6815832 | solution.py:318
  7.5 5.3 %all-to-all-start.6 = ((bf16[8,2,384,128]{3,2,1,0:T(8,128)(2,1)}), bf16[8,2,384,128]{3,2,1,0:T(8,128)(2,1)}, u32[]{:S(2)}, u32[]{:S(2)}) async-start(bf16[8,2,384,128]{3,2,1,0:T(8,128)(2,1)} %get-tuple-element.131), calls=%async_computation.6 | async-start | bytes 3145728 | tf_op jit(solution)/shard_map/cond/branch_6_fun/all_to_all | solution.py:21
  12.8 3.3 %collective-permute-start.11 = (bf16[256,1024]{1,0:T(8,128)(2,1)}, bf16[256,1024]{1,0:T(8,128)(2,1)}, u32[]{:S(2)}, u32[]{:S(2)}) collective-permute-start(bf16[256,1024]{1,0:T(8,128)(2,1)} %get-tuple-element.130), channel_id=1, source_target_pairs={{0,64},{8,72},{16,80},{24,88},{32,96},{40,104},{48,112},{56,120},{... | collective-permute-start | bytes 1572872 | tf_op jit(solution)/shard_map/cond/branch_6_fun/ppermute | solution.py:28
  16.1 25.3 %collective-permute-done.11 = bf16[256,1024]{1,0:T(8,128)(2,1)} collective-permute-done((bf16[256,1024]{1,0:T(8,128)(2,1)}, bf16[256,1024]{1,0:T(8,128)(2,1)}, u32[]{:S(2)}, u32[]{:S(2)}) %collective-permute-start.11) | collective-permute-done | bytes 524320 | tf_op jit(solution)/shard_map/cond/branch_6_fun/ppermute | solution.py:28
  41.4 0.0 all-to-all-done.6
  41.4 0.0 copy-start.8
  41.4 0.0 copy-start.6
  41.4 0.0 copy-start.7
  41.4 2.6 %project_query.1.query_ref = bf16[8,256,128]{2,1,0:T(8,128)(2,1)} custom-call(bf16[256,1024]{1,0:T(8,128)(2,1)} %get-tuple-element.145.tokens_ref, bf16[1024,1024]{1,0:T(8,128)(2,1)S(1)} %get-tuple-element.146.w_ref), custom_call_target="tpu_custom_call" | custom-call | flops 536870912 | bytes 2097152 | tf_op jit(solution)/shard_map/project_query/pallas_call | solution.py:111
  44.0 5.4 %all-to-all-start.9 = ((bf16[8,256,128]{2,1,0:T(8,128)(2,1)}), bf16[8,256,128]{2,1,0:T(8,128)(2,1)S(1)}, u32[]{:S(2)}, u32[]{:S(2)}) async-start(bf16[8,256,128]{2,1,0:T(8,128)(2,1)} %project_query.1.query_ref), calls=%async_computation.9 | async-start | bytes 1048576 | tf_op jit(solution)/shard_map/all_to_all | solution.py:21
  49.5 0.0 copy-done.8
  49.5 0.1 pad.2.clone
  49.6 0.0 copy-done.6
  49.6 0.0 copy-done.7
  49.6 0.2 fusion.meta_ref
  49.8 9.5 %all-to-all-done.9.query_ref = bf16[8,256,128]{2,1,0:T(8,128)(2,1)S(1)} async-done(((bf16[8,256,128]{2,1,0:T(8,128)(2,1)}), bf16[8,256,128]{2,1,0:T(8,128)(2,1)S(1)}, u32[]{:S(2)}, u32[]{:S(2)}) %all-to-all-start.9) | async-done | bytes 524320 | tf_op jit(solution)/shard_map/all_to_all | solution.py:21
  59.3 10.3 %attend.1 = bf16[8,256,128]{2,1,0:T(8,128)(2,1)} custom-call(s32[3]{0:T(128)S(1)} %fusion.meta_ref, bf16[8,256,128]{2,1,0:T(8,128)(2,1)S(1)} %all-to-all-done.9.query_ref, bf16[8,2,384,128]{3,2,1,0:T(8,128)(2,1)} %get-tuple-element.147.cache_ref), custom_call_target="tpu_custom_call" | custom-call | flops 3221225472 | bytes 1572864 | tf_op jit(solution)/shard_map/attend/pallas_call | solution.py:237
  69.5 3.5 %all-to-all-start.10 = ((bf16[8,256,128]{2,1,0:T(8,128)(2,1)}), bf16[8,256,128]{2,1,0:T(8,128)(2,1)S(1)}, u32[]{:S(2)}, u32[]{:S(2)}) async-start(bf16[8,256,128]{2,1,0:T(8,128)(2,1)} %attend.1), calls=%async_computation.10 | async-start | bytes 1048576 | tf_op jit(solution)/shard_map/all_to_all | solution.py:21
  73.0 0.0 copy-start
  73.0 0.0 copy-start.5
  73.1 5.8 %project_own.1 = (f32[256,1024]{1,0:T(8,128)S(1)}, f32[8,256,128]{2,1,0:T(8,128)S(1)}) custom-call(bf16[256,1024]{1,0:T(8,128)(2,1)} %get-tuple-element.145.tokens_ref, bf16[8,256,128]{2,1,0:T(8,128)(2,1)} %project_query.1.query_ref, bf16[1024,4096]{1,0:T(8,128)(2,1)} %wk_ref.1, bf16[1024,4096]{1,0:T(8,128)(2,1)} %wk_ref.1, bf16[1024,4096]{1,0:T(8,128)(2,1)} %wk_ref.1), custom_call_target="tpu_custom_call" | custom-call | flops 1610612736 | bytes 6291456 | tf_op jit(solution)/shard_map/project_own/pallas_call | solution.py:142
  78.8 0.0 copy-start.1
  78.8 1.0 %copy-done.1 = f32[256,1024]{1,0:T(8,128)} copy-done((f32[256,1024]{1,0:T(8,128)}, f32[256,1024]{1,0:T(8,128)S(1)}, u32[]{:S(2)}) %copy-start.1) | copy-done | bytes 1048600
  79.8 0.0 copy-start.3
  79.8 1.0 %copy-done.3 = f32[8,256,128]{2,1,0:T(8,128)} copy-done((f32[8,256,128]{2,1,0:T(8,128)}, f32[8,256,128]{2,1,0:T(8,128)S(1)}, u32[]{:S(2)}) %copy-start.3) | copy-done | bytes 1048600
  80.9 0.8 all-to-all-done.10.mixed_ref
  81.7 0.0 copy-done
  81.7 0.0 copy-done.5
  81.7 0.0 copy-start.2
  81.7 1.2 %copy-done.2 = f32[256,1024]{1,0:T(8,128)S(1)} copy-done((f32[256,1024]{1,0:T(8,128)S(1)}, f32[256,1024]{1,0:T(8,128)}, u32[]{:S(2)}) %copy-start.2) | copy-done | bytes 1048600
  82.9 0.0 copy-start.4
  82.9 1.2 %copy-done.4 = f32[8,256,128]{2,1,0:T(8,128)S(1)} copy-done((f32[8,256,128]{2,1,0:T(8,128)S(1)}, f32[8,256,128]{2,1,0:T(8,128)}, u32[]{:S(2)}) %copy-start.4) | copy-done | bytes 1048600
  84.1 2.4 %finish.1 = bf16[256,1024]{1,0:T(8,128)(2,1)} custom-call(s32[3]{0:T(128)S(1)} %fusion.meta_ref, bf16[8,256,128]{2,1,0:T(8,128)(2,1)S(1)} %all-to-all-done.10.mixed_ref, f32[8,256,128]{2,1,0:T(8,128)S(1)} %copy-done.4, f32[256,1024]{1,0:T(8,128)S(1)} %copy-done.2, f32[1,1024]{1,0:T(1,128)S(1)} %bitcast.9, bf16[1024,1024]{1,0:T(8,128)(2,1)S(1)} %copy-done), custom_call_target="tpu_custom_call" | custom-call | flops 536870912 | bytes 2097152 | tf_op jit(solution)/shard_map/finish/pallas_call | solution.py:279
  (1 shorter events, 0.0 us)
Async XLA Ops:
  7.5 33.9 %all-to-all-start.6 = ((bf16[8,2,384,128]{3,2,1,0:T(8,128)(2,1)}), bf16[8,2,384,128]{3,2,1,0:T(8,128)(2,1)}, u32[]{:S(2)}, u32[]{:S(2)}) async-start(bf16[8,2,384,128]{3,2,1,0:T(8,128)(2,1)} %get-tuple-element.131), calls=%async_computation.6 | async-start | bytes 3145728 | tf_op jit(solution)/shard_map/cond/branch_6_fun/all_to_all | solution.py:21
  12.8 28.6 %collective-permute-start.11 = (bf16[256,1024]{1,0:T(8,128)(2,1)}, bf16[256,1024]{1,0:T(8,128)(2,1)}, u32[]{:S(2)}, u32[]{:S(2)}) collective-permute-start(bf16[256,1024]{1,0:T(8,128)(2,1)} %get-tuple-element.130), channel_id=1, source_target_pairs={{0,64},{8,72},{16,80},{24,88},{32,96},{40,104},{48,112},{56,120},{... | collective-permute-start | bytes 1572872 | tf_op jit(solution)/shard_map/cond/branch_6_fun/ppermute | solution.py:28
  41.4 8.1 %copy-start.8 = (s32[32]{0:T(128)S(1)}, s32[32]{0:T(128)}, u32[]{:S(2)}) copy-start(s32[32]{0:T(128)} %param.29) | copy-start | bytes 388
  41.4 8.2 %copy-start.6 = (s32[32]{0:T(128)S(1)}, s32[32]{0:T(128)}, u32[]{:S(2)}) copy-start(s32[32]{0:T(128)} %param.31) | copy-start | bytes 388
  41.4 8.2 %copy-start.7 = (s32[32]{0:T(128)S(1)}, s32[32]{0:T(128)}, u32[]{:S(2)}) copy-start(s32[32]{0:T(128)} %param.30) | copy-start | bytes 388
  44.0 15.2 %all-to-all-start.9 = ((bf16[8,256,128]{2,1,0:T(8,128)(2,1)}), bf16[8,256,128]{2,1,0:T(8,128)(2,1)S(1)}, u32[]{:S(2)}, u32[]{:S(2)}) async-start(bf16[8,256,128]{2,1,0:T(8,128)(2,1)} %project_query.1.query_ref), calls=%async_computation.9 | async-start | bytes 1048576 | tf_op jit(solution)/shard_map/all_to_all | solution.py:21
  69.5 12.1 %all-to-all-start.10 = ((bf16[8,256,128]{2,1,0:T(8,128)(2,1)}), bf16[8,256,128]{2,1,0:T(8,128)(2,1)S(1)}, u32[]{:S(2)}, u32[]{:S(2)}) async-start(bf16[8,256,128]{2,1,0:T(8,128)(2,1)} %attend.1), calls=%async_computation.10 | async-start | bytes 1048576 | tf_op jit(solution)/shard_map/all_to_all | solution.py:21
  73.0 8.6 %copy-start = (bf16[1024,1024]{1,0:T(8,128)(2,1)S(1)}, bf16[1024,1024]{1,0:T(8,128)(2,1)}, u32[]{:S(2)}) copy-start(bf16[1024,1024]{1,0:T(8,128)(2,1)} %w_ref.1) | copy-start | bytes 6291460
  73.0 8.6 %copy-start.5 = (f32[1024]{0:T(1024)S(1)}, f32[1024]{0:T(1024)}, u32[]{:S(2)}) copy-start(f32[1024]{0:T(1024)} %param.28) | copy-start | bytes 12292
  78.8 1.0 %copy-start.1 = (f32[256,1024]{1,0:T(8,128)}, f32[256,1024]{1,0:T(8,128)S(1)}, u32[]{:S(2)}) copy-start(f32[256,1024]{1,0:T(8,128)S(1)} %get-tuple-element.149.gate_ref) | copy-start | bytes 3145732
  79.8 1.0 %copy-start.3 = (f32[8,256,128]{2,1,0:T(8,128)}, f32[8,256,128]{2,1,0:T(8,128)S(1)}, u32[]{:S(2)}) copy-start(f32[8,256,128]{2,1,0:T(8,128)S(1)} %get-tuple-element.148.own_ref) | copy-start | bytes 3145732
  81.7 1.2 %copy-start.2 = (f32[256,1024]{1,0:T(8,128)S(1)}, f32[256,1024]{1,0:T(8,128)}, u32[]{:S(2)}) copy-start(f32[256,1024]{1,0:T(8,128)} %copy-done.1) | copy-start | bytes 3145732
  82.9 1.2 %copy-start.4 = (f32[8,256,128]{2,1,0:T(8,128)S(1)}, f32[8,256,128]{2,1,0:T(8,128)}, u32[]{:S(2)}) copy-start(f32[8,256,128]{2,1,0:T(8,128)} %copy-done.3) | copy-start | bytes 3145732
where the time goes:
time: 87.1 us; the launch traced here: 86.5 us
  waiting for transfers between devices  35.6 us (41%)
  Pallas kernels  24.5 us (28%)
  starting transfers between devices  17.5 us (20%)
  local copies, waits for them, and re-layouts  6.42 us (7%)
  between operations  2.14 us (2%)
    ppermute x1, waiting for transfers between devices, rotate(): return lax.ppermute(value, 'group', pairs)  25.3 us
    all_to_all x3, starting transfers between devices, exchange(): return lax.all_to_all(value, 'helper', 0, 0, tiled=True)  14.2 us
    all_to_all x3, waiting for transfers between devices, exchange(): return lax.all_to_all(value, 'helper', 0, 0, tiled=True)  10.3 us
    pallas_call x1, Pallas kernels, attend(): pl.pallas_call(functools.partial(attend_kernel, head ** (-0.5), rows, chu...  10.3 us
    pallas_call x1, Pallas kernels, project_own(): pl.pallas_call(functools.partial(own_kernel, head ** (-0.5)), grid=(steps...  5.77 us
    unnamed x18, local copies, waits for them, and re-layouts  4.49 us
    pallas_call x1, Pallas kernels, prepare(): pl.pallas_call(prepare_kernel, in_specs=[pl.BlockSpec(memory_space=pltpu....  3.5 us
    ppermute x1, starting transfers between devices, rotate(): return lax.ppermute(value, 'group', pairs)  3.27 us
  transfers between devices with their start and end apart: 4, of which 3 were waited for; matrix products, arithmetic and copies ran while one was open for 0% of the time, Pallas kernels for 7%

commit v1 on v0

v1 whole, which is shorter than its diff:
```python
import functools

import jax
import jax.numpy as jnp
from jax import lax
from jax.experimental import pallas as pl
from jax.experimental.pallas import tpu as pltpu
from jax.sharding import PartitionSpec as P


HEADS = 8
FAR = 4


def silu(value):
    half = 0.5 * value
    return half + half * jnp.tanh(half)


def exchange(value):
    return lax.all_to_all(value, "helper", 0, 0, tiled=True)


def rotate(value, steps, count):
    if steps % count == 0:
        return value
    pairs = [(source, (source + steps) % count) for source in range(count)]
    return lax.ppermute(value, "group", pairs)


def near_move(steps, count, head):
    def move(tokens, cache, w_uvqk):
        moved = rotate(tokens, steps, count)
        split, w_query = prepare(cache, w_uvqk, head)
        return moved, split, w_query

    return move


def far_move(steps, count, head):
    def move(tokens, split, w_query):
        moved = rotate(tokens, steps, count)
        cache = exchange(split)
        kept, query = project_query(moved, w_query, head)
        return kept, cache, query

    return move


def route(offset, groups):
    half = groups // 2
    bits = FAR.bit_length() - 1
    far = jnp.where(
        offset <= half - FAR,
        offset >> bits,
        jnp.where(offset < half + FAR, half // FAR, (offset + FAR - 1) >> bits),
    )
    return offset - FAR * far, far


def limit(mebibytes):
    return pltpu.CompilerParams(vmem_limit_bytes=mebibytes << 20)


def prepare_kernel(cache_ref, w_uvqk_ref, split_ref, query_ref, buf, reads, writes, sem):
    heads, _, _, head = split_ref.shape
    width = query_ref.shape[1]

    def pull(h):
        cols = pl.ds(pl.multiple_of(h * head, head), head)
        return pltpu.make_async_copy(cache_ref.at[:, :, cols], buf.at[h], reads.at[h])

    def push(h):
        return pltpu.make_async_copy(buf.at[h], split_ref.at[h], writes.at[h])

    def each(step):
        def body(h, carry):
            step(h)
            return carry

        lax.fori_loop(0, heads, body, 0)

    def pass_on(h):
        pull(h).wait()
        push(h).start()

    weights = pltpu.make_async_copy(w_uvqk_ref.at[:, 2 * width : 3 * width], query_ref, sem)
    each(lambda h: pull(h).start())
    weights.start()
    each(pass_on)
    each(lambda h: push(h).wait())
    weights.wait()


def prepare(cache, w_uvqk, head):
    two, length, width = cache.shape
    heads = width // head
    shape = (heads, two, length, head)
    return pl.pallas_call(
        prepare_kernel,
        in_specs=[pl.BlockSpec(memory_space=pltpu.HBM), pl.BlockSpec(memory_space=pltpu.HBM)],
        out_specs=[pl.BlockSpec(memory_space=pltpu.HBM), pl.BlockSpec(memory_space=pltpu.VMEM)],
        out_shape=[
            jax.ShapeDtypeStruct(shape, cache.dtype),
            pltpu.VMEM((width, width), w_uvqk.dtype),
        ],
        scratch_shapes=[
            pltpu.VMEM(shape, cache.dtype),
            pltpu.SemaphoreType.DMA((heads,)),
            pltpu.SemaphoreType.DMA((heads,)),
            pltpu.SemaphoreType.DMA,
        ],
        compiler_params=limit(3),
        name="prepare",
    )(cache, w_uvqk)


def query_kernel(tokens_ref, w_ref, kept_ref, out_ref, sem):
    heads, _, head = out_ref.shape
    keep = pltpu.make_async_copy(tokens_ref, kept_ref, sem)
    keep.start()
    tokens = tokens_ref[...]
    for h in range(0, heads, 2):
        cols = slice(h * head, (h + 2) * head)
        proj = jnp.dot(tokens, w_ref[:, cols], preferred_element_type=jnp.float32)
        proj = silu(proj).astype(jnp.bfloat16)
        out_ref[h] = proj[:, :head]
        out_ref[h + 1] = proj[:, head:]
    keep.wait()


def project_query(tokens, w_query, head):
    slots, width = tokens.shape
    heads = width // head
    whole = pl.BlockSpec(memory_space=pltpu.VMEM)
    return pl.pallas_call(
        query_kernel,
        in_specs=[whole, whole],
        out_specs=[pl.BlockSpec(memory_space=pltpu.HBM), whole],
        out_shape=[
            jax.ShapeDtypeStruct(tokens.shape, tokens.dtype),
            jax.ShapeDtypeStruct((heads, slots, head), jnp.bfloat16),
        ],
        scratch_shapes=[pltpu.SemaphoreType.DMA],
        cost_estimate=pl.CostEstimate(
            flops=2 * slots * width * width, bytes_accessed=2 * width * width, transcendentals=slots * width
        ),
        compiler_params=limit(8),
        name="project_query",
    )(tokens, w_query)


def own_kernel(scale, pieces, tokens_ref, query_ref, gain_ref, w_ref, gate_ref, own_ref, weights, sems):
    heads, _, head = query_ref.shape
    width = heads * head
    cols = width // pieces
    per = cols // head
    places = (0, 1, 3)

    def pull(piece, part):
        first = places[part] * width + piece * cols
        return pltpu.make_async_copy(
            w_ref.at[:, first : first + cols],
            weights.at[part, :, piece * cols : (piece + 1) * cols],
            sems.at[piece, part],
        )

    for piece in range(pieces):
        for part in (1, 2, 0):
            pull(piece, part).start()
    tokens = tokens_ref[...]

    def project(piece, part):
        pull(piece, part).wait()
        here = weights[part, :, piece * cols : (piece + 1) * cols]
        return silu(jnp.dot(tokens, here, preferred_element_type=jnp.float32))

    for piece in range(pieces):
        here = slice(piece * cols, (piece + 1) * cols)
        own_v = project(piece, 1).astype(jnp.bfloat16)
        own_k = project(piece, 2).astype(jnp.bfloat16)
        gate_ref[:, here] = (project(piece, 0) * gain_ref[:, here]).astype(gate_ref.dtype)
        for h in range(per):
            part = slice(h * head, (h + 1) * head)
            query = query_ref[piece * per + h].astype(jnp.float32)
            score = jnp.sum(query * own_k[:, part].astype(jnp.float32), axis=-1, keepdims=True) * scale
            weight = silu(score).astype(jnp.bfloat16).astype(jnp.float32)
            term = weight * own_v[:, part].astype(jnp.float32)
            own_ref[piece * per + h] = term.astype(own_ref.dtype)


def project_own(tokens, query, gain, w_uvqk, head):
    slots, width = tokens.shape
    heads = width // head
    pieces = 2
    whole = pl.BlockSpec(memory_space=pltpu.VMEM)
    return pl.pallas_call(
        functools.partial(own_kernel, head ** (-0.5), pieces),
        in_specs=[whole, whole, whole, pl.BlockSpec(memory_space=pltpu.HBM)],
        out_specs=[whole, whole],
        out_shape=[
            pltpu.VMEM((slots, width), jnp.bfloat16),
            pltpu.VMEM((heads, slots, head), jnp.bfloat16),
        ],
        scratch_shapes=[
            pltpu.VMEM((3, width, width), w_uvqk.dtype),
            pltpu.SemaphoreType.DMA((pieces, 3)),
        ],
        cost_estimate=pl.CostEstimate(
            flops=6 * slots * width * width, bytes_accessed=6 * width * width, transcendentals=3 * slots * width
        ),
        compiler_params=limit(14),
        name="project_own",
    )(tokens, query, gain.reshape(1, width), w_uvqk)


def visible_kernel(meta_ref, cache_ref, keys_ref, values_ref, sems):
    shards, length, head = keys_ref.shape
    visible = meta_ref[1]
    key_copy = pltpu.make_async_copy(cache_ref.at[:, 0], keys_ref, sems.at[0])
    value_copy = pltpu.make_async_copy(cache_ref.at[:, 1], values_ref, sems.at[1])
    key_copy.start()
    value_copy.start()
    key_copy.wait()
    for shard in range(shards):

        @pl.when(visible < (shard + 1) * length)
        def _():
            place = shard * length + lax.broadcasted_iota(jnp.int32, (length, head), 0)
            keys = keys_ref[shard].astype(jnp.float32)
            keys_ref[shard] = jnp.where(place < visible, keys, 0.0).astype(jnp.bfloat16)

    value_copy.wait()


def visible_prefix(meta, cache):
    shards, _, length, head = cache.shape
    kept = pltpu.VMEM((shards, length, head), cache.dtype)
    return pl.pallas_call(
        visible_kernel,
        in_specs=[pl.BlockSpec(memory_space=pltpu.SMEM), pl.BlockSpec(memory_space=pl.ANY)],
        out_specs=[pl.BlockSpec(memory_space=pltpu.VMEM), pl.BlockSpec(memory_space=pltpu.VMEM)],
        out_shape=[kept, kept],
        scratch_shapes=[pltpu.SemaphoreType.DMA((2,))],
        compiler_params=limit(1),
        name="visible_prefix",
    )(meta, cache)


def attend_kernel(scale, rows, chunk, groups, meta_ref, query_ref, keys_ref, values_ref, out_ref):
    blocks, slots, head = query_ref.shape
    shards, length, _ = keys_ref.shape
    per = rows // slots
    count = meta_ref[0]
    visible = meta_ref[1]
    live_blocks = jnp.minimum((count + rows - 1) // rows, blocks // per)

    def attend_to(used):
        span = used * length
        pieces = span // chunk

        def row_block(number, carry):
            first = number * per
            query = query_ref[pl.ds(first, per)].reshape(rows, head)
            query = (query.astype(jnp.float32) * (0.5 * scale)).astype(jnp.bfloat16)
            keys = keys_ref[:used].reshape(span, head)
            values = values_ref[:used].reshape(span, head)

            def scores(piece):
                part = keys[piece * chunk : (piece + 1) * chunk]
                return lax.dot_general(
                    query, part, (((1,), (1,)), ((), ())), preferred_element_type=jnp.float32
                )

            acc = jnp.zeros((rows, head), jnp.float32)
            ahead = scores(0)
            for piece in range(pieces):
                half = ahead.astype(jnp.bfloat16)
                if piece + 1 < pieces:
                    ahead = scores(piece + 1)
                weight = half + half * jnp.tanh(half)
                part = values[piece * chunk : (piece + 1) * chunk]
                acc = acc + jnp.dot(weight, part, preferred_element_type=jnp.float32)
            out_ref[pl.ds(first, per)] = acc.astype(jnp.bfloat16).reshape(per, slots, head)
            return carry

        lax.fori_loop(0, live_blocks, row_block, 0)

    below = 0
    for used in groups:
        within = visible > below * length
        if used < shards:
            within = jnp.logical_and(within, visible <= used * length)
        pl.when(within)(functools.partial(attend_to, used))
        below = used

    def dead_block(number, carry):
        out_ref[pl.ds(number * per, per)] = jnp.zeros((per, slots, head), jnp.bfloat16)
        return carry

    lax.fori_loop(live_blocks, blocks // per, dead_block, 0)


def attend(meta, query, keys, values):
    blocks, slots, head = query.shape
    shards, length, _ = keys.shape
    rows = 4 * slots
    groups = (shards // 2, shards)
    flops = 4 * blocks * slots * shards * length * head
    whole = pl.BlockSpec(memory_space=pltpu.VMEM)
    return pl.pallas_call(
        functools.partial(attend_kernel, head ** (-0.5), rows, length, groups),
        in_specs=[pl.BlockSpec(memory_space=pltpu.SMEM), whole, whole, whole],
        out_specs=whole,
        out_shape=jax.ShapeDtypeStruct(query.shape, jnp.bfloat16),
        cost_estimate=pl.CostEstimate(
            flops=flops, bytes_accessed=keys.size * 4, transcendentals=blocks * slots * shards * length
        ),
        compiler_params=limit(14),
        name="attend",
    )(meta, query, keys, values)


def finish_kernel(pieces, meta_ref, mixed_ref, own_ref, gate_ref, w_ref, out_ref):
    heads, slots, head = mixed_ref.shape
    count = meta_ref[0]
    first = meta_ref[2] * slots
    width = heads * head
    rows = slots // pieces
    for piece in range(pieces):
        here = slice(piece * rows, (piece + 1) * rows)
        mixed = jnp.concatenate(
            [
                mixed_ref[h, here].astype(jnp.float32) + own_ref[h, here].astype(jnp.float32)
                for h in range(heads)
            ],
            axis=1,
        )
        centre = mixed - jnp.sum(mixed, axis=-1, keepdims=True) * (1.0 / width)
        spread = jnp.sum(centre * centre, axis=-1, keepdims=True) * (1.0 / width)
        normed = centre * lax.rsqrt(spread + 1e-05) * gate_ref[here].astype(jnp.float32)
        result = jnp.dot(normed.astype(jnp.bfloat16), w_ref[...], preferred_element_type=jnp.float32)
        place = first + piece * rows + lax.broadcasted_iota(jnp.int32, result.shape, 0)
        out_ref[here] = jnp.where(place < count, result, 0.0).astype(jnp.bfloat16)


def finish(meta, mixed, own, gate, w_output):
    slots, width = gate.shape
    whole = pl.BlockSpec(memory_space=pltpu.VMEM)
    return pl.pallas_call(
        functools.partial(finish_kernel, 2),
        in_specs=[pl.BlockSpec(memory_space=pltpu.SMEM)] + [whole] * 4,
        out_specs=whole,
        out_shape=jax.ShapeDtypeStruct((slots, width), jnp.bfloat16),
        cost_estimate=pl.CostEstimate(
            flops=2 * slots * width * width, bytes_accessed=2 * width * width, transcendentals=slots
        ),
        compiler_params=limit(10),
        name="finish",
    )(meta, mixed, own, gate, w_output)


def local(candidates, prefix_cache, w_uvqk, w_output, norm_gain, owner, counts, prefix_len):
    groups = lax.axis_size("group")
    group_here = lax.axis_index("group")
    helper_here = lax.axis_index("helper")
    offset = jnp.minimum(lax.optimization_barrier(owner[0]), groups - 1)
    width = candidates.shape[2]
    head = width // HEADS
    near, far = route(offset, groups)
    nears = range(1 - FAR, FAR)
    fars = range(groups // FAR + 1)
    near_moves = [near_move(steps, groups, head) for steps in nears]
    far_moves = [far_move(FAR * steps, groups, head) for steps in fars]
    w_uvqk = pltpu.with_memory_space_constraint(w_uvqk, pltpu.HBM)
    prefix = pltpu.with_memory_space_constraint(prefix_cache[0], pltpu.HBM)
    tokens, split, w_query = lax.switch(near + FAR - 1, near_moves, candidates[0], prefix, w_uvqk)
    tokens, cache, query = lax.switch(far, far_moves, tokens, split, w_query)
    user = (group_here - offset) % groups
    table = jnp.stack([counts, prefix_len, jnp.full_like(counts, helper_here)])
    places = lax.broadcasted_iota(jnp.int32, table.shape, 1)
    meta = jnp.sum(jnp.where(places == user, table, 0), axis=1)
    query_all = exchange(query)
    gate, own = project_own(tokens, query, norm_gain, w_uvqk, head)
    keys, values = visible_prefix(meta, cache)
    heads_out = attend(meta, query_all, keys, values)
    mixed = exchange(heads_out)
    return finish(meta, mixed, own, gate, w_output)[None]


def solution(mesh):
    in_specs = (
        P("group", "helper", None),
        P("group", None, "helper", None),
        P(),
        P(),
        P(),
        P(),
        P(),
        P(),
    )
    out_specs = P("group", "helper", None)
    return jax.shard_map(local, mesh=mesh, in_specs=in_specs, out_specs=out_specs, check_vma=False)
```

time: 87.1 us -> 80.8 us (0.928)
  local copies, waits for them, and re-layouts: 6.42 us -> 3.79 us
  Pallas kernels: 24.5 us -> 22.7 us
  between operations: 2.14 us -> 0.76 us
    unnamed x18 -> x12, local copies, waits for them, and re-layouts: 4.49 us -> 1.85 us
    pallas_call x4 -> x5, Pallas kernels: 21 us -> 19.8 us  [the longest x1 8.25 us: attend(): pl.pallas_call(functools.partial(attend_kernel, head ** (-0.5), rows, len...]
  transfers between devices with their start and end apart: 4 -> 4, of which waited for: 3 -> 3; matrix products, arithmetic and copies ran while one was open for 0% -> 0% of each run, Pallas kernels for 7% -> 11%
where the time goes in v1:
time: 80.8 us; the launch traced here: 80.3 us
  waiting for transfers between devices  35 us (43%)
  Pallas kernels  22.7 us (28%)
  starting transfers between devices  17.5 us (22%)
  local copies, waits for them, and re-layouts  3.79 us (5%)
    ppermute x1, waiting for transfers between devices, rotate(): return lax.ppermute(value, 'group', pairs)  25.2 us
    all_to_all x3, starting transfers between devices, exchange(): return lax.all_to_all(value, 'helper', 0, 0, tiled=True)  14.3 us
    all_to_all x3, waiting for transfers between devices, exchange(): return lax.all_to_all(value, 'helper', 0, 0, tiled=True)  9.79 us
    pallas_call x1, Pallas kernels, attend(): pl.pallas_call(functools.partial(attend_kernel, head ** (-0.5), rows, len...  8.25 us
    pallas_call x1, Pallas kernels, project_own(): pl.pallas_call(functools.partial(own_kernel, head ** (-0.5), pieces), in_...  5.62 us
    ppermute x1, starting transfers between devices, rotate(): return lax.ppermute(value, 'group', pairs)  3.27 us
    pallas_call x1, Pallas kernels, prepare(): pl.pallas_call(prepare_kernel, in_specs=[pl.BlockSpec(memory_space=pltpu....  2.96 us
    pallas_call x1, Pallas kernels, finish(): pl.pallas_call(functools.partial(finish_kernel, 2), in_specs=[pl.BlockSpe...  2.33 us
  transfers between devices with their start and end apart: 4, of which 3 were waited for; matrix products, arithmetic and copies ran while one was open for 0% of the time, Pallas kernels for 11%

profile of v1, /device:TPU:32, one launch (start us, length us, event | category | flops | bytes accessed | tf_op | source)
XLA Modules:
  0.0 80.3 jit_solution(15911141257915917102)
XLA Ops:
  0.7 4.9 %conditional.2 = (bf16[256,1024]{1,0:T(8,128)(2,1)}, bf16[8,2,384,128]{3,2,1,0:T(8,128)(2,1)}, bf16[1024,1024]{1,0:T(8,128)(2,1)S(1)}) conditional(s32[]{:T(128)} %clamp.7, (bf16[256,1024]{1,0:T(8,128)(2,1)}, bf16[2,384,1024]{2,1,0:T(8,128)(2,1)}, bf16[1024,4096]{1,0:T(8,128)(2,1)}) %tuple.95, ...), branch_computations={%region_1.2_spmd, %region_2.3_spmd, %region_3.4_spmd, %region_4.5_... | conditional | bytes 2097216 | solution.py:377
  0.7 1.9 %copy.18 = bf16[256,1024]{1,0:T(8,128)(2,1)} copy(bf16[256,1024]{1,0:T(8,128)(2,1)} %get-tuple-element.210) | data formatting | bytes 1048576 | tf_op jit(solution)/shard_map/cond
  2.6 3.0 %prepare.10 = (bf16[8,2,384,128]{3,2,1,0:T(8,128)(2,1)}, bf16[1024,1024]{1,0:T(8,128)(2,1)S(1)}) custom-call(bf16[2,384,1024]{2,1,0:T(8,128)(2,1)} %get-tuple-element.117.cache_ref, bf16[1024,4096]{1,0:T(8,128)(2,1)} %get-tuple-element.118.w_uvqk_ref), custom_call_target="tpu_custom_call" | custom-call | tf_op jit(solution)/shard_map/cond/branch_3_fun/prepare/pallas_call | solution.py:99
  5.6 0.0 copy-start.4
  5.6 0.0 copy-start.5
  5.6 35.7 %conditional.3 = (bf16[256,1024]{1,0:T(8,128)(2,1)}, bf16[8,2,384,128]{3,2,1,0:T(8,128)(2,1)}, bf16[8,256,128]{2,1,0:T(8,128)(2,1)}) conditional(s32[]{:T(128)} %clamp.6, (bf16[256,1024]{1,0:T(8,128)(2,1)}, bf16[1024,1024]{1,0:T(8,128)(2,1)S(1)}, bf16[8,2,384,128]{3,2,1,0:T(8,128)(2,1)}) %tuple.71, ...), branch_computations={%region_8.9_spmd, %region_9.10_spmd, %region_10.11_spmd, %region_1... | conditional | flops 536870912 | bytes 8912992 | solution.py:378
  5.6 5.3 %all-to-all-start.2 = ((bf16[8,2,384,128]{3,2,1,0:T(8,128)(2,1)}), bf16[8,2,384,128]{3,2,1,0:T(8,128)(2,1)}, u32[]{:S(2)}, u32[]{:S(2)}) async-start(bf16[8,2,384,128]{3,2,1,0:T(8,128)(2,1)} %get-tuple-element.149), calls=%async_computation.2 | async-start | bytes 3145728 | tf_op jit(solution)/shard_map/cond/branch_2_fun/all_to_all | solution.py:21
  10.9 3.3 %collective-permute-start.7 = (bf16[256,1024]{1,0:T(8,128)(2,1)}, bf16[256,1024]{1,0:T(8,128)(2,1)S(1)}, u32[]{:S(2)}, u32[]{:S(2)}) collective-permute-start(bf16[256,1024]{1,0:T(8,128)(2,1)} %get-tuple-element.146), channel_id=1, source_target_pairs={{0,64},{8,72},{16,80},{24,88},{32,96},{40,104},{48,112},{56,120},{... | collective-permute-start | bytes 1572872 | tf_op jit(solution)/shard_map/cond/branch_2_fun/ppermute | solution.py:28
  14.2 25.2 %collective-permute-done.7.tokens_ref = bf16[256,1024]{1,0:T(8,128)(2,1)S(1)} collective-permute-done((bf16[256,1024]{1,0:T(8,128)(2,1)}, bf16[256,1024]{1,0:T(8,128)(2,1)S(1)}, u32[]{:S(2)}, u32[]{:S(2)}) %collective-permute-start.7) | collective-permute-done | bytes 524320 | tf_op jit(solution)/shard_map/cond/branch_2_fun/ppermute | solution.py:28
  39.4 1.6 %project_query.11 = (bf16[256,1024]{1,0:T(8,128)(2,1)}, bf16[8,256,128]{2,1,0:T(8,128)(2,1)}) custom-call(bf16[256,1024]{1,0:T(8,128)(2,1)S(1)} %collective-permute-done.7.tokens_ref, bf16[1024,1024]{1,0:T(8,128)(2,1)S(1)} %get-tuple-element.147.w_ref), custom_call_target="tpu_custom_call" | custom-call | flops 536870912 | bytes 2097152 | tf_op jit(solution)/shard_map/cond/branch_2_fun/project_query/pallas_call | solution.py:136
  41.1 0.0 all-to-all-done.2
  41.3 5.4 %all-to-all-start.9 = ((bf16[8,256,128]{2,1,0:T(8,128)(2,1)}), bf16[8,256,128]{2,1,0:T(8,128)(2,1)S(1)}, u32[]{:S(2)}, u32[]{:S(2)}) async-start(bf16[8,256,128]{2,1,0:T(8,128)(2,1)} %get-tuple-element.194.query_ref), calls=%async_computation.9 | async-start | bytes 1048576 | tf_op jit(solution)/shard_map/all_to_all | solution.py:21
  46.8 0.1 pad.2.clone
  46.8 0.0 copy-done.4
  46.8 0.0 copy-done.5
  46.8 0.2 fusion.meta_ref
  47.0 1.9 %visible_prefix.1 = (bf16[8,384,128]{2,1,0:T(8,128)(2,1)S(1)}, bf16[8,384,128]{2,1,0:T(8,128)(2,1)S(1)}) custom-call(s32[3]{0:T(128)S(1)} %fusion.meta_ref, bf16[8,2,384,128]{3,2,1,0:T(8,128)(2,1)} %get-tuple-element.195.cache_ref), custom_call_target="tpu_custom_call" | custom-call | tf_op jit(solution)/shard_map/visible_prefix/pallas_call | solution.py:239
  49.0 7.6 %all-to-all-done.9.query_ref = bf16[8,256,128]{2,1,0:T(8,128)(2,1)S(1)} async-done(((bf16[8,256,128]{2,1,0:T(8,128)(2,1)}), bf16[8,256,128]{2,1,0:T(8,128)(2,1)S(1)}, u32[]{:S(2)}, u32[]{:S(2)}) %all-to-all-start.9) | async-done | bytes 524320 | tf_op jit(solution)/shard_map/all_to_all | solution.py:21
  56.6 0.0 copy-start.3
  56.6 8.2 %attend.1 = bf16[8,256,128]{2,1,0:T(8,128)(2,1)} custom-call(s32[3]{0:T(128)S(1)} %fusion.meta_ref, bf16[8,256,128]{2,1,0:T(8,128)(2,1)S(1)} %all-to-all-done.9.query_ref, bf16[8,384,128]{2,1,0:T(8,128)(2,1)S(1)} %get-tuple-element.196.keys_ref, bf16[8,384,128]{2,1,0:T(8,128)(2,1)S(1)} %get-tuple-element.197.values_ref), custom_call_target="tpu_custom_call" | custom-call | flops 3221225472 | bytes 1572864 | tf_op jit(solution)/shard_map/attend/pallas_call | solution.py:311
  64.8 3.5 %all-to-all-start.10 = ((bf16[8,256,128]{2,1,0:T(8,128)(2,1)}), bf16[8,256,128]{2,1,0:T(8,128)(2,1)S(1)}, u32[]{:S(2)}, u32[]{:S(2)}) async-start(bf16[8,256,128]{2,1,0:T(8,128)(2,1)} %attend.1), calls=%async_computation.10 | async-start | bytes 1048576 | tf_op jit(solution)/shard_map/all_to_all | solution.py:21
  68.3 0.0 copy-done.3
  68.3 0.0 copy-start
  68.4 5.6 %project_own.1 = (bf16[256,1024]{1,0:T(8,128)(2,1)S(1)}, bf16[8,256,128]{2,1,0:T(8,128)(2,1)S(1)}) custom-call(bf16[256,1024]{1,0:T(8,128)(2,1)} %get-tuple-element.198.tokens_ref, bf16[8,256,128]{2,1,0:T(8,128)(2,1)} %get-tuple-element.194.query_ref, f32[1,1024]{1,0:T(1,128)S(1)} %bitcast.9, bf16[1024,4096]{1,0:T(8,128)(2,1)} %w_ref.2), custom_call_target="tpu_custom_call" | custom-call | flops 1610612736 | bytes 6291456 | tf_op jit(solution)/shard_map/project_own/pallas_call | solution.py:197
  74.0 0.0 copy-start.1
  74.0 0.8 copy-done.1
  74.8 2.2 %all-to-all-done.10.mixed_ref = bf16[8,256,128]{2,1,0:T(8,128)(2,1)S(1)} async-done(((bf16[8,256,128]{2,1,0:T(8,128)(2,1)}), bf16[8,256,128]{2,1,0:T(8,128)(2,1)S(1)}, u32[]{:S(2)}, u32[]{:S(2)}) %all-to-all-start.10) | async-done | bytes 524320 | tf_op jit(solution)/shard_map/all_to_all | solution.py:21
  77.0 0.0 copy-done
  77.0 0.0 copy-start.2
  77.0 1.0 %copy-done.2 = bf16[8,256,128]{2,1,0:T(8,128)(2,1)S(1)} copy-done((bf16[8,256,128]{2,1,0:T(8,128)(2,1)S(1)}, bf16[8,256,128]{2,1,0:T(8,128)(2,1)}, u32[]{:S(2)}) %copy-start.2) | copy-done | bytes 524312
  78.0 2.3 %finish.1 = bf16[256,1024]{1,0:T(8,128)(2,1)} custom-call(s32[3]{0:T(128)S(1)} %fusion.meta_ref, bf16[8,256,128]{2,1,0:T(8,128)(2,1)S(1)} %all-to-all-done.10.mixed_ref, bf16[8,256,128]{2,1,0:T(8,128)(2,1)S(1)} %copy-done.2, bf16[256,1024]{1,0:T(8,128)(2,1)S(1)} %get-tuple-element.200.gate_ref, bf16[1024,1024]{1,0:T(8,128)(2,1)S(1)} %copy-done), custom_call_target="tpu_custom_call" | custom-call | flops 536870912 | bytes 2097152 | tf_op jit(solution)/shard_map/finish/pallas_call | solution.py:350
  (1 shorter events, 0.0 us)
Async XLA Ops:
  5.6 41.3 %copy-start.4 = (s32[32]{0:T(128)S(1)}, s32[32]{0:T(128)}, u32[]{:S(2)}) copy-start(s32[32]{0:T(128)} %param.31) | copy-start | bytes 388
  5.6 41.3 %copy-start.5 = (s32[32]{0:T(128)S(1)}, s32[32]{0:T(128)}, u32[]{:S(2)}) copy-start(s32[32]{0:T(128)} %param.30) | copy-start | bytes 388
  5.6 35.5 %all-to-all-start.2 = ((bf16[8,2,384,128]{3,2,1,0:T(8,128)(2,1)}), bf16[8,2,384,128]{3,2,1,0:T(8,128)(2,1)}, u32[]{:S(2)}, u32[]{:S(2)}) async-start(bf16[8,2,384,128]{3,2,1,0:T(8,128)(2,1)} %get-tuple-element.149), calls=%async_computation.2 | async-start | bytes 3145728 | tf_op jit(solution)/shard_map/cond/branch_2_fun/all_to_all | solution.py:21
  10.9 28.5 %collective-permute-start.7 = (bf16[256,1024]{1,0:T(8,128)(2,1)}, bf16[256,1024]{1,0:T(8,128)(2,1)S(1)}, u32[]{:S(2)}, u32[]{:S(2)}) collective-permute-start(bf16[256,1024]{1,0:T(8,128)(2,1)} %get-tuple-element.146), channel_id=1, source_target_pairs={{0,64},{8,72},{16,80},{24,88},{32,96},{40,104},{48,112},{56,120},{... | collective-permute-start | bytes 1572872 | tf_op jit(solution)/shard_map/cond/branch_2_fun/ppermute | solution.py:28
  41.3 15.3 %all-to-all-start.9 = ((bf16[8,256,128]{2,1,0:T(8,128)(2,1)}), bf16[8,256,128]{2,1,0:T(8,128)(2,1)S(1)}, u32[]{:S(2)}, u32[]{:S(2)}) async-start(bf16[8,256,128]{2,1,0:T(8,128)(2,1)} %get-tuple-element.194.query_ref), calls=%async_computation.9 | async-start | bytes 1048576 | tf_op jit(solution)/shard_map/all_to_all | solution.py:21
  56.6 11.8 %copy-start.3 = (f32[1024]{0:T(1024)S(1)}, f32[1024]{0:T(1024)}, u32[]{:S(2)}) copy-start(f32[1024]{0:T(1024)} %param.28) | copy-start | bytes 12292
  64.8 12.1 %all-to-all-start.10 = ((bf16[8,256,128]{2,1,0:T(8,128)(2,1)}), bf16[8,256,128]{2,1,0:T(8,128)(2,1)S(1)}, u32[]{:S(2)}, u32[]{:S(2)}) async-start(bf16[8,256,128]{2,1,0:T(8,128)(2,1)} %attend.1), calls=%async_computation.10 | async-start | bytes 1048576 | tf_op jit(solution)/shard_map/all_to_all | solution.py:21
  68.3 8.6 %copy-start = (bf16[1024,1024]{1,0:T(8,128)(2,1)S(1)}, bf16[1024,1024]{1,0:T(8,128)(2,1)}, u32[]{:S(2)}) copy-start(bf16[1024,1024]{1,0:T(8,128)(2,1)} %w_ref.3) | copy-start | bytes 6291460
  74.0 0.8 copy-start.1
  77.0 1.0 %copy-start.2 = (bf16[8,256,128]{2,1,0:T(8,128)(2,1)S(1)}, bf16[8,256,128]{2,1,0:T(8,128)(2,1)}, u32[]{:S(2)}) copy-start(bf16[8,256,128]{2,1,0:T(8,128)(2,1)} %copy-done.1) | copy-start | bytes 1572868

commit v2 on v1

--- a/solution.py
+++ b/solution.py
@@ -28,8 +28,11 @@
     return lax.ppermute(value, "group", pairs)
 
 
-def near_move(steps, count, head):
+def first_move(steps, count, head):
     def move(tokens, cache, w_uvqk):
+        if steps == 0:
+            split, w_query, moved = prepare(cache, w_uvqk, head, tokens)
+            return moved, split, w_query
         moved = rotate(tokens, steps, count)
         split, w_query = prepare(cache, w_uvqk, head)
         return moved, split, w_query
@@ -37,7 +40,7 @@
     return move
 
 
-def far_move(steps, count, head):
+def second_move(steps, count, head):
     def move(tokens, split, w_query):
         moved = rotate(tokens, steps, count)
         cache = exchange(split)
@@ -47,72 +50,112 @@
     return move
 
 
-def route(offset, groups):
-    half = groups // 2
-    bits = FAR.bit_length() - 1
-    far = jnp.where(
-        offset <= half - FAR,
-        offset >> bits,
-        jnp.where(offset < half + FAR, half // FAR, (offset + FAR - 1) >> bits),
-    )
-    return offset - FAR * far, far
+def plan(groups):
+    steps = []
+    for offset in range(groups):
+        signed = (offset + groups // 2 - 1) % groups - groups // 2 + 1
+        size, sign = abs(signed), 1 if signed > 0 else -1
+        if size < FAR:
+            steps.append((0, signed))
+            continue
+        far = groups // 2 if size >= groups // 2 - FAR else size // FAR * FAR
+        steps.append((sign * (size - far), sign * far if far < groups // 2 else far))
+    firsts = sorted({first for first, _ in steps})
+    seconds = sorted({second for _, second in steps})
+    return firsts, seconds, [(firsts.index(x), seconds.index(y)) for x, y in steps]
+
+
+def pick_int(values, index):
+    runs = []
+    at = 0
+    while at < len(values):
+        slope = values[at + 1] - values[at] if at + 1 < len(values) else 0
+        end = at + 1
+        while end < len(values) and values[end] - values[end - 1] == slope:
+            end += 1
+        runs.append((at, values[at], slope))
+        at = end
+    out = None
+    for start, value, slope in runs:
+        line = value + slope * (index - start) if slope else jnp.int32(value)
+        out = line if out is None else jnp.where(index >= start, line, out)
+    return out
 
 
 def limit(mebibytes):
     return pltpu.CompilerParams(vmem_limit_bytes=mebibytes << 20)
 
 
-def prepare_kernel(cache_ref, w_uvqk_ref, split_ref, query_ref, buf, reads, writes, sem):
-    heads, _, _, head = split_ref.shape
-    width = query_ref.shape[1]
-
-    def pull(h):
-        cols = pl.ds(pl.multiple_of(h * head, head), head)
-        return pltpu.make_async_copy(cache_ref.at[:, :, cols], buf.at[h], reads.at[h])
-
-    def push(h):
-        return pltpu.make_async_copy(buf.at[h], split_ref.at[h], writes.at[h])
-
-    def each(step):
-        def body(h, carry):
-            step(h)
-            return carry
-
-        lax.fori_loop(0, heads, body, 0)
-
-    def pass_on(h):
-        pull(h).wait()
-        push(h).start()
-
-    weights = pltpu.make_async_copy(w_uvqk_ref.at[:, 2 * width : 3 * width], query_ref, sem)
-    each(lambda h: pull(h).start())
-    weights.start()
-    each(pass_on)
-    each(lambda h: push(h).wait())
-    weights.wait()
-
-
-def prepare(cache, w_uvqk, head):
+def prepare(cache, w_uvqk, head, tokens=None):
     two, length, width = cache.shape
     heads = width // head
     shape = (heads, two, length, head)
-    return pl.pallas_call(
-        prepare_kernel,
-        in_specs=[pl.BlockSpec(memory_space=pltpu.HBM), pl.BlockSpec(memory_space=pltpu.HBM)],
-        out_specs=[pl.BlockSpec(memory_space=pltpu.HBM), pl.BlockSpec(memory_space=pltpu.VMEM)],
-        out_shape=[
-            jax.ShapeDtypeStruct(shape, cache.dtype),
-            pltpu.VMEM((width, width), w_uvqk.dtype),
-        ],
-        scratch_shapes=[
-            pltpu.VMEM(shape, cache.dtype),
-            pltpu.SemaphoreType.DMA((heads,)),
-            pltpu.SemaphoreType.DMA((heads,)),
-            pltpu.SemaphoreType.DMA,
-        ],
-        compiler_params=limit(3),
+    far = pl.BlockSpec(memory_space=pltpu.HBM)
+    near = pl.BlockSpec(memory_space=pltpu.VMEM)
+
+    def kernel(*refs):
+        if tokens is None:
+            cache_ref, w_ref, split_ref, query_ref, buf, reads, writes, sem = refs
+        else:
+            cache_ref, w_ref, tokens_ref, split_ref, query_ref, kept_ref, buf, reads, writes, sem, held, moves = refs
+            pull_tokens = pltpu.make_async_copy(tokens_ref, held, moves.at[0])
+            push_tokens = pltpu.make_async_copy(held, kept_ref, moves.at[1])
+
+        def pull(h):
+            cols = pl.ds(pl.multiple_of(h * head, head), head)
+            return pltpu.make_async_copy(cache_ref.at[:, :, cols], buf.at[h], reads.at[h])
+
+        def push(h):
+            return pltpu.make_async_copy(buf.at[h], split_ref.at[h], writes.at[h])
+
+        def each(step):
+            def body(h, carry):
+                step(h)
+                return carry
+
+            lax.fori_loop(0, heads, body, 0)
+
+        def pass_on(h):
+            pull(h).wait()
+            push(h).start()
+
+        weights = pltpu.make_async_copy(w_ref.at[:, 2 * width : 3 * width], query_ref, sem)
+        if tokens is not None:
+            pull_tokens.start()
+        each(lambda h: pull(h).start())
+        weights.start()
+        if tokens is not None:
+            pull_tokens.wait()
+            push_tokens.start()
+        each(pass_on)
+        each(lambda h: push(h).wait())
+        weights.wait()
+        if tokens is not None:
+            push_tokens.wait()
+
+    operands = [cache, w_uvqk]
+    out_specs = [far, near]
+    out_shape = [pltpu.HBM(shape, cache.dtype), pltpu.VMEM((width, width), w_uvqk.dtype)]
+    scratch = [
+        pltpu.VMEM(shape, cache.dtype),
+        pltpu.SemaphoreType.DMA((heads,)),
+        pltpu.SemaphoreType.DMA((heads,)),
+        pltpu.SemaphoreType.DMA,
+    ]
+    if tokens is not None:
+        operands.append(tokens)
+        out_specs.append(far)
+        out_shape.append(pltpu.HBM(tokens.shape, tokens.dtype))
+        scratch += [pltpu.VMEM(tokens.shape, tokens.dtype), pltpu.SemaphoreType.DMA((2,))]
+    return pl.pallas_call(
+        kernel,
+        in_specs=[far] * len(operands),
+        out_specs=out_specs,
+        out_shape=out_shape,
+        scratch_shapes=scratch,
+        compiler_params=limit(4),
         name="prepare",
-    )(cache, w_uvqk)
+    )(*operands)
 
 
 def query_kernel(tokens_ref, w_ref, kept_ref, out_ref, sem):
@@ -120,12 +163,17 @@
     keep = pltpu.make_async_copy(tokens_ref, kept_ref, sem)
     keep.start()
     tokens = tokens_ref[...]
-    for h in range(0, heads, 2):
-        cols = slice(h * head, (h + 2) * head)
+    per = heads // 2
+
+    def some_heads(part, carry):
+        cols = pl.ds(pl.multiple_of(part * per * head, head), per * head)
         proj = jnp.dot(tokens, w_ref[:, cols], preferred_element_type=jnp.float32)
         proj = silu(proj).astype(jnp.bfloat16)
-        out_ref[h] = proj[:, :head]
-        out_ref[h + 1] = proj[:, head:]
+        for h in range(per):
+            out_ref[part * per + h] = proj[:, h * head : (h + 1) * head]
+        return carry
+
+    lax.fori_loop(0, 2, some_heads, 0)
     keep.wait()
 
 
@@ -138,7 +186,7 @@
         in_specs=[whole, whole],
         out_specs=[pl.BlockSpec(memory_space=pltpu.HBM), whole],
         out_shape=[
-            jax.ShapeDtypeStruct(tokens.shape, tokens.dtype),
+            pltpu.HBM(tokens.shape, tokens.dtype),
             jax.ShapeDtypeStruct((heads, slots, head), jnp.bfloat16),
         ],
         scratch_shapes=[pltpu.SemaphoreType.DMA],
@@ -247,52 +295,34 @@
     )(meta, cache)
 
 
-def attend_kernel(scale, rows, chunk, groups, meta_ref, query_ref, keys_ref, values_ref, out_ref):
+def attend_kernel(scale, rows, meta_ref, query_ref, keys_ref, values_ref, out_ref):
     blocks, slots, head = query_ref.shape
-    shards, length, _ = keys_ref.shape
+    shards, _, _ = keys_ref.shape
     per = rows // slots
-    count = meta_ref[0]
-    visible = meta_ref[1]
-    live_blocks = jnp.minimum((count + rows - 1) // rows, blocks // per)
-
-    def attend_to(used):
-        span = used * length
-        pieces = span // chunk
-
-        def row_block(number, carry):
-            first = number * per
-            query = query_ref[pl.ds(first, per)].reshape(rows, head)
-            query = (query.astype(jnp.float32) * (0.5 * scale)).astype(jnp.bfloat16)
-            keys = keys_ref[:used].reshape(span, head)
-            values = values_ref[:used].reshape(span, head)
-
-            def scores(piece):
-                part = keys[piece * chunk : (piece + 1) * chunk]
-                return lax.dot_general(
-                    query, part, (((1,), (1,)), ((), ())), preferred_element_type=jnp.float32
-                )
-
-            acc = jnp.zeros((rows, head), jnp.float32)
-            ahead = scores(0)
-            for piece in range(pieces):
-                half = ahead.astype(jnp.bfloat16)
-                if piece + 1 < pieces:
-                    ahead = scores(piece + 1)
-                weight = half + half * jnp.tanh(half)
-                part = values[piece * chunk : (piece + 1) * chunk]
-                acc = acc + jnp.dot(weight, part, preferred_element_type=jnp.float32)
-            out_ref[pl.ds(first, per)] = acc.astype(jnp.bfloat16).reshape(per, slots, head)
-            return carry
-
-        lax.fori_loop(0, live_blocks, row_block, 0)
-
-    below = 0
-    for used in groups:
-        within = visible > below * length
-        if used < shards:
-            within = jnp.logical_and(within, visible <= used * length)
-        pl.when(within)(functools.partial(attend_to, used))
-        below = used
+    live_blocks = jnp.minimum((meta_ref[0] + rows - 1) // rows, blocks // per)
+
+    def row_block(number, carry):
+        first = number * per
+        query = query_ref[pl.ds(first, per)].reshape(rows, head)
+        query = (query.astype(jnp.float32) * (0.5 * scale)).astype(jnp.bfloat16)
+
+        def scores(shard):
+            return lax.dot_general(
+                query, keys_ref[shard], (((1,), (1,)), ((), ())), preferred_element_type=jnp.float32
+            )
+
+        acc = jnp.zeros((rows, head), jnp.float32)
+        ahead = scores(0)
+        for shard in range(shards):
+            half = ahead.astype(jnp.bfloat16)
+            if shard + 1 < shards:
+                ahead = scores(shard + 1)
+            weight = half + half * jnp.tanh(half)
+            acc = acc + jnp.dot(weight, values_ref[shard], preferred_element_type=jnp.float32)
+        out_ref[pl.ds(first, per)] = acc.astype(jnp.bfloat16).reshape(per, slots, head)
+        return carry
+
+    lax.fori_loop(0, live_blocks, row_block, 0)
 
     def dead_block(number, carry):
         out_ref[pl.ds(number * per, per)] = jnp.zeros((per, slots, head), jnp.bfloat16)
@@ -305,11 +335,10 @@
     blocks, slots, head = query.shape
     shards, length, _ = keys.shape
     rows = 4 * slots
-    groups = (shards // 2, shards)
     flops = 4 * blocks * slots * shards * length * head
     whole = pl.BlockSpec(memory_space=pltpu.VMEM)
     return pl.pallas_call(
-        functools.partial(attend_kernel, head ** (-0.5), rows, length, groups),
+        functools.partial(attend_kernel, head ** (-0.5), rows),
         in_specs=[pl.BlockSpec(memory_space=pltpu.SMEM), whole, whole, whole],
         out_specs=whole,
         out_shape=jax.ShapeDtypeStruct(query.shape, jnp.bfloat16),
@@ -321,12 +350,13 @@
     )(meta, query, keys, values)
 
 
-def finish_kernel(pieces, meta_ref, mixed_ref, own_ref, gate_ref, w_ref, out_ref):
+def finish_kernel(pieces, meta_ref, mixed_ref, own_ref, gate_ref, w_ref, out_ref, buf, sems):
     heads, slots, head = mixed_ref.shape
     count = meta_ref[0]
     first = meta_ref[2] * slots
     width = heads * head
     rows = slots // pieces
+    copies = []
     for piece in range(pieces):
         here = slice(piece * rows, (piece + 1) * rows)
         mixed = jnp.concatenate(
@@ -341,16 +371,22 @@
         normed = centre * lax.rsqrt(spread + 1e-05) * gate_ref[here].astype(jnp.float32)
         result = jnp.dot(normed.astype(jnp.bfloat16), w_ref[...], preferred_element_type=jnp.float32)
         place = first + piece * rows + lax.broadcasted_iota(jnp.int32, result.shape, 0)
-        out_ref[here] = jnp.where(place < count, result, 0.0).astype(jnp.bfloat16)
+        buf[here] = jnp.where(place < count, result, 0.0).astype(jnp.bfloat16)
+        copies.append(pltpu.make_async_copy(buf.at[here], out_ref.at[here], sems.at[piece]))
+        copies[-1].start()
+    for copy in copies:
+        copy.wait()
 
 
 def finish(meta, mixed, own, gate, w_output):
     slots, width = gate.shape
+    pieces = 2
     whole = pl.BlockSpec(memory_space=pltpu.VMEM)
     return pl.pallas_call(
-        functools.partial(finish_kernel, 2),
+        functools.partial(finish_kernel, pieces),
         in_specs=[pl.BlockSpec(memory_space=pltpu.SMEM)] + [whole] * 4,
-        out_specs=whole,
+        out_specs=pl.BlockSpec(memory_space=pltpu.HBM),
+        scratch_shapes=[pltpu.VMEM((slots, width), jnp.bfloat16), pltpu.SemaphoreType.DMA((pieces,))],
         out_shape=jax.ShapeDtypeStruct((slots, width), jnp.bfloat16),
         cost_estimate=pl.CostEstimate(
             flops=2 * slots * width * width, bytes_accessed=2 * width * width, transcendentals=slots
@@ -367,15 +403,15 @@
     offset = jnp.minimum(lax.optimization_barrier(owner[0]), groups - 1)
     width = candidates.shape[2]
     head = width // HEADS
-    near, far = route(offset, groups)
-    nears = range(1 - FAR, FAR)
-    fars = range(groups // FAR + 1)
-    near_moves = [near_move(steps, groups, head) for steps in nears]
-    far_moves = [far_move(FAR * steps, groups, head) for steps in fars]
+    firsts, seconds, steps = plan(groups)
+    first = pick_int([x for x, _ in steps], offset)
+    second = pick_int([y for _, y in steps], offset)
+    first_moves = [first_move(by, groups, head) for by in firsts]
+    second_moves = [second_move(by, groups, head) for by in seconds]
     w_uvqk = pltpu.with_memory_space_constraint(w_uvqk, pltpu.HBM)
     prefix = pltpu.with_memory_space_constraint(prefix_cache[0], pltpu.HBM)
-    tokens, split, w_query = lax.switch(near + FAR - 1, near_moves, candidates[0], prefix, w_uvqk)
-    tokens, cache, query = lax.switch(far, far_moves, tokens, split, w_query)
+    tokens, split, w_query = lax.switch(first, first_moves, candidates[0], prefix, w_uvqk)
+    tokens, cache, query = lax.switch(second, second_moves, tokens, split, w_query)
     user = (group_here - offset) % groups
     table = jnp.stack([counts, prefix_len, jnp.full_like(counts, helper_here)])
     places = lax.broadcasted_iota(jnp.int32, table.shape, 1)

time: 80.8 us -> 81.1 us (level)
  local copies, waits for them, and re-layouts: 3.79 us -> 1.93 us
  waiting for transfers between devices: 35 us -> 36.6 us
    cond x1 -> x0, local copies, waits for them, and re-layouts: 1.87 us -> none
    all_to_all x3, waiting for transfers between devices: 9.79 us -> 11.3 us  [exchange(): return lax.all_to_all(value, 'helper', 0, 0, tiled=True)]
  transfers between devices with their start and end apart: 4 -> 4, of which waited for: 3 -> 3; matrix products, arithmetic and copies ran while one was open for 0% -> 0% of each run, Pallas kernels for 11% -> 12%
where the time goes in v2:
time: 81.1 us; the launch traced here: 80.7 us
  waiting for transfers between devices  36.6 us (45%)
  Pallas kernels  23 us (28%)
  starting transfers between devices  17.8 us (22%)
  local copies, waits for them, and re-layouts  1.93 us (2%)
  between operations  0.97 us (1%)
    ppermute x1, waiting for transfers between devices, rotate(): return lax.ppermute(value, 'group', pairs)  25.2 us
    all_to_all x3, starting transfers between devices, exchange(): return lax.all_to_all(value, 'helper', 0, 0, tiled=True)  14.5 us
    all_to_all x3, waiting for transfers between devices, exchange(): return lax.all_to_all(value, 'helper', 0, 0, tiled=True)  11.3 us
    pallas_call x1, Pallas kernels, attend(): pl.pallas_call(functools.partial(attend_kernel, head ** (-0.5), rows), in...  8.26 us
    pallas_call x1, Pallas kernels, project_own(): pl.pallas_call(functools.partial(own_kernel, head ** (-0.5), pieces), in_...  5.62 us
    ppermute x1, starting transfers between devices, rotate(): return lax.ppermute(value, 'group', pairs)  3.27 us
    pallas_call x1, Pallas kernels, prepare(): pl.pallas_call(kernel, in_specs=[far] * len(operands), out_specs=out_spec...  3.14 us
    pallas_call x1, Pallas kernels, finish(): pl.pallas_call(functools.partial(finish_kernel, pieces), in_specs=[pl.Blo...  2.25 us
  transfers between devices with their start and end apart: 4, of which 3 were waited for; matrix products, arithmetic and copies ran while one was open for 0% of the time, Pallas kernels for 12%

profile of v2, /device:TPU:32, one launch (start us, length us, event | category | flops | bytes accessed | tf_op | source)
XLA Modules:
  0.0 80.7 jit_solution(92823989697487166)
XLA Ops:
  0.7 3.2 %conditional.2 = (bf16[256,1024]{1,0:T(8,128)(2,1)}, bf16[8,2,384,128]{3,2,1,0:T(8,128)(2,1)}, bf16[1024,1024]{1,0:T(8,128)(2,1)S(1)}) conditional(s32[]{:T(128)} %clamp.7, (bf16[256,1024]{1,0:T(8,128)(2,1)}, bf16[2,384,1024]{2,1,0:T(8,128)(2,1)}, bf16[1024,4096]{1,0:T(8,128)(2,1)}) %tuple.122, ...), branch_computations={%region_1.2_spmd, %region_2.3_spmd, %region_3.4_spmd, %region_4.5_... | conditional | bytes 2097216 | solution.py:413
  0.7 3.1 %prepare.13 = (bf16[8,2,384,128]{3,2,1,0:T(8,128)(2,1)}, bf16[1024,1024]{1,0:T(8,128)(2,1)S(1)}, bf16[256,1024]{1,0:T(8,128)(2,1)}) custom-call(bf16[2,384,1024]{2,1,0:T(8,128)(2,1)} %get-tuple-element.151.refs_0_, bf16[1024,4096]{1,0:T(8,128)(2,1)} %get-tuple-element.152.refs_1_, bf16[256,1024]{1,0:T(8,128)(2,1)} %get-tuple-element.153.refs_2_), custom_call_target="tpu_custom_call" | custom-call | tf_op jit(solution)/shard_map/cond/branch_4_fun/prepare/pallas_call | solution.py:150
  3.9 0.0 copy-start.4
  3.9 0.0 copy-start.5
  3.9 35.9 %conditional.3 = (bf16[256,1024]{1,0:T(8,128)(2,1)}, bf16[8,2,384,128]{3,2,1,0:T(8,128)(2,1)}, bf16[8,256,128]{2,1,0:T(8,128)(2,1)}) conditional(s32[]{:T(128)} %clamp.6, (bf16[256,1024]{1,0:T(8,128)(2,1)}, bf16[1024,1024]{1,0:T(8,128)(2,1)S(1)}, bf16[8,2,384,128]{3,2,1,0:T(8,128)(2,1)}) %tuple.91, ...), branch_computations={%region_10.11_spmd, %region_11.12_spmd, %region_12.13_spmd, %regio... | conditional | flops 536870912 | bytes 8912992 | solution.py:414
  4.1 5.3 %all-to-all-start.10 = ((bf16[8,2,384,128]{3,2,1,0:T(8,128)(2,1)}), bf16[8,2,384,128]{3,2,1,0:T(8,128)(2,1)}, u32[]{:S(2)}, u32[]{:S(2)}) async-start(bf16[8,2,384,128]{3,2,1,0:T(8,128)(2,1)} %get-tuple-element.230), calls=%async_computation.10 | async-start | bytes 3145728 | tf_op jit(solution)/shard_map/cond/branch_10_fun/all_to_all | solution.py:21
  9.5 3.3 %collective-permute-start.17 = (bf16[256,1024]{1,0:T(8,128)(2,1)}, bf16[256,1024]{1,0:T(8,128)(2,1)S(1)}, u32[]{:S(2)}, u32[]{:S(2)}) collective-permute-start(bf16[256,1024]{1,0:T(8,128)(2,1)} %get-tuple-element.227), channel_id=1, source_target_pairs={{0,64},{8,72},{16,80},{24,88},{32,96},{40,104},{48,112},{56,120},{... | collective-permute-start | bytes 1572872 | tf_op jit(solution)/shard_map/cond/branch_10_fun/ppermute | solution.py:28
  12.7 25.2 %collective-permute-done.17.tokens_ref = bf16[256,1024]{1,0:T(8,128)(2,1)S(1)} collective-permute-done((bf16[256,1024]{1,0:T(8,128)(2,1)}, bf16[256,1024]{1,0:T(8,128)(2,1)S(1)}, u32[]{:S(2)}, u32[]{:S(2)}) %collective-permute-start.17) | collective-permute-done | bytes 524320 | tf_op jit(solution)/shard_map/cond/branch_10_fun/ppermute | solution.py:28
  38.0 1.8 %project_query.22 = (bf16[256,1024]{1,0:T(8,128)(2,1)}, bf16[8,256,128]{2,1,0:T(8,128)(2,1)}) custom-call(bf16[256,1024]{1,0:T(8,128)(2,1)S(1)} %collective-permute-done.17.tokens_ref, bf16[1024,1024]{1,0:T(8,128)(2,1)S(1)} %get-tuple-element.228.w_ref), custom_call_target="tpu_custom_call" | custom-call | flops 536870912 | bytes 2097152 | tf_op jit(solution)/shard_map/cond/branch_10_fun/project_query/pallas_call | solution.py:184
  39.8 0.0 all-to-all-done.10
  39.8 5.4 %all-to-all-start.12 = ((bf16[8,256,128]{2,1,0:T(8,128)(2,1)}), bf16[8,256,128]{2,1,0:T(8,128)(2,1)S(1)}, u32[]{:S(2)}, u32[]{:S(2)}) async-start(bf16[8,256,128]{2,1,0:T(8,128)(2,1)} %get-tuple-element.250.query_ref), calls=%async_computation.12 | async-start | bytes 1048576 | tf_op jit(solution)/shard_map/all_to_all | solution.py:21
  45.3 0.1 pad.2.clone
  45.3 0.0 copy-done.4
  45.3 0.0 copy-done.5
  45.3 0.2 fusion.meta_ref
  45.5 1.9 %visible_prefix.1 = (bf16[8,384,128]{2,1,0:T(8,128)(2,1)S(1)}, bf16[8,384,128]{2,1,0:T(8,128)(2,1)S(1)}) custom-call(s32[3]{0:T(128)S(1)} %fusion.meta_ref, bf16[8,2,384,128]{3,2,1,0:T(8,128)(2,1)} %get-tuple-element.251.cache_ref), custom_call_target="tpu_custom_call" | custom-call | tf_op jit(solution)/shard_map/visible_prefix/pallas_call | solution.py:287
  47.5 7.6 %all-to-all-done.12.query_ref = bf16[8,256,128]{2,1,0:T(8,128)(2,1)S(1)} async-done(((bf16[8,256,128]{2,1,0:T(8,128)(2,1)}), bf16[8,256,128]{2,1,0:T(8,128)(2,1)S(1)}, u32[]{:S(2)}, u32[]{:S(2)}) %all-to-all-start.12) | async-done | bytes 524320 | tf_op jit(solution)/shard_map/all_to_all | solution.py:21
  55.1 0.0 copy-start.3
  55.1 8.3 %attend.1 = bf16[8,256,128]{2,1,0:T(8,128)(2,1)} custom-call(s32[3]{0:T(128)S(1)} %fusion.meta_ref, bf16[8,256,128]{2,1,0:T(8,128)(2,1)S(1)} %all-to-all-done.12.query_ref, bf16[8,384,128]{2,1,0:T(8,128)(2,1)S(1)} %get-tuple-element.252.keys_ref, bf16[8,384,128]{2,1,0:T(8,128)(2,1)S(1)} %get-tuple-element.253.values_ref), custom_call_target="tpu_custom_call" | custom-call | flops 3221225472 | bytes 1572864 | tf_op jit(solution)/shard_map/attend/pallas_call | solution.py:340
  63.3 3.7 %all-to-all-start.13 = ((bf16[8,256,128]{2,1,0:T(8,128)(2,1)}), bf16[8,256,128]{2,1,0:T(8,128)(2,1)S(1)}, u32[]{:S(2)}, u32[]{:S(2)}) async-start(bf16[8,256,128]{2,1,0:T(8,128)(2,1)} %attend.1), calls=%async_computation.13 | async-start | bytes 1048576 | tf_op jit(solution)/shard_map/all_to_all | solution.py:21
  67.1 0.0 copy-done.3
  67.1 0.0 copy-start
  67.1 5.6 %project_own.1 = (bf16[256,1024]{1,0:T(8,128)(2,1)S(1)}, bf16[8,256,128]{2,1,0:T(8,128)(2,1)S(1)}) custom-call(bf16[256,1024]{1,0:T(8,128)(2,1)} %get-tuple-element.254.tokens_ref, bf16[8,256,128]{2,1,0:T(8,128)(2,1)} %get-tuple-element.250.query_ref, f32[1,1024]{1,0:T(1,128)S(1)} %bitcast.9, bf16[1024,4096]{1,0:T(8,128)(2,1)} %w_ref.2), custom_call_target="tpu_custom_call" | custom-call | flops 1610612736 | bytes 6291456 | tf_op jit(solution)/shard_map/project_own/pallas_call | solution.py:245
  72.7 0.0 copy-start.1
  72.7 0.8 copy-done.1
  73.5 3.7 %all-to-all-done.13.mixed_ref = bf16[8,256,128]{2,1,0:T(8,128)(2,1)S(1)} async-done(((bf16[8,256,128]{2,1,0:T(8,128)(2,1)}), bf16[8,256,128]{2,1,0:T(8,128)(2,1)S(1)}, u32[]{:S(2)}, u32[]{:S(2)}) %all-to-all-start.13) | async-done | bytes 524320 | tf_op jit(solution)/shard_map/all_to_all | solution.py:21
  77.2 0.0 copy-done
  77.2 0.0 copy-start.2
  77.2 1.0 %copy-done.2 = bf16[8,256,128]{2,1,0:T(8,128)(2,1)S(1)} copy-done((bf16[8,256,128]{2,1,0:T(8,128)(2,1)S(1)}, bf16[8,256,128]{2,1,0:T(8,128)(2,1)}, u32[]{:S(2)}) %copy-start.2) | copy-done | bytes 524312
  78.3 2.3 %finish.1 = bf16[256,1024]{1,0:T(8,128)(2,1)} custom-call(s32[3]{0:T(128)S(1)} %fusion.meta_ref, bf16[8,256,128]{2,1,0:T(8,128)(2,1)S(1)} %all-to-all-done.13.mixed_ref, bf16[8,256,128]{2,1,0:T(8,128)(2,1)S(1)} %copy-done.2, bf16[256,1024]{1,0:T(8,128)(2,1)S(1)} %get-tuple-element.256.gate_ref, bf16[1024,1024]{1,0:T(8,128)(2,1)S(1)} %copy-done), custom_call_target="tpu_custom_call" | custom-call | flops 536870912 | bytes 2097152 | tf_op jit(solution)/shard_map/finish/pallas_call | solution.py:385
  (1 shorter events, 0.0 us)
Async XLA Ops:
  3.9 41.4 %copy-start.4 = (s32[32]{0:T(128)S(1)}, s32[32]{0:T(128)}, u32[]{:S(2)}) copy-start(s32[32]{0:T(128)} %param.36) | copy-start | bytes 388
  3.9 41.4 %copy-start.5 = (s32[32]{0:T(128)S(1)}, s32[32]{0:T(128)}, u32[]{:S(2)}) copy-start(s32[32]{0:T(128)} %param.35) | copy-start | bytes 388
  4.1 35.6 %all-to-all-start.10 = ((bf16[8,2,384,128]{3,2,1,0:T(8,128)(2,1)}), bf16[8,2,384,128]{3,2,1,0:T(8,128)(2,1)}, u32[]{:S(2)}, u32[]{:S(2)}) async-start(bf16[8,2,384,128]{3,2,1,0:T(8,128)(2,1)} %get-tuple-element.230), calls=%async_computation.10 | async-start | bytes 3145728 | tf_op jit(solution)/shard_map/cond/branch_10_fun/all_to_all | solution.py:21
  9.5 28.5 %collective-permute-start.17 = (bf16[256,1024]{1,0:T(8,128)(2,1)}, bf16[256,1024]{1,0:T(8,128)(2,1)S(1)}, u32[]{:S(2)}, u32[]{:S(2)}) collective-permute-start(bf16[256,1024]{1,0:T(8,128)(2,1)} %get-tuple-element.227), channel_id=1, source_target_pairs={{0,64},{8,72},{16,80},{24,88},{32,96},{40,104},{48,112},{56,120},{... | collective-permute-start | bytes 1572872 | tf_op jit(solution)/shard_map/cond/branch_10_fun/ppermute | solution.py:28
  39.8 15.3 %all-to-all-start.12 = ((bf16[8,256,128]{2,1,0:T(8,128)(2,1)}), bf16[8,256,128]{2,1,0:T(8,128)(2,1)S(1)}, u32[]{:S(2)}, u32[]{:S(2)}) async-start(bf16[8,256,128]{2,1,0:T(8,128)(2,1)} %get-tuple-element.250.query_ref), calls=%async_computation.12 | async-start | bytes 1048576 | tf_op jit(solution)/shard_map/all_to_all | solution.py:21
  55.1 12.0 %copy-start.3 = (f32[1024]{0:T(1024)S(1)}, f32[1024]{0:T(1024)}, u32[]{:S(2)}) copy-start(f32[1024]{0:T(1024)} %param.33) | copy-start | bytes 12292
  63.3 13.9 %all-to-all-start.13 = ((bf16[8,256,128]{2,1,0:T(8,128)(2,1)}), bf16[8,256,128]{2,1,0:T(8,128)(2,1)S(1)}, u32[]{:S(2)}, u32[]{:S(2)}) async-start(bf16[8,256,128]{2,1,0:T(8,128)(2,1)} %attend.1), calls=%async_computation.13 | async-start | bytes 1048576 | tf_op jit(solution)/shard_map/all_to_all | solution.py:21
  67.1 10.2 %copy-start = (bf16[1024,1024]{1,0:T(8,128)(2,1)S(1)}, bf16[1024,1024]{1,0:T(8,128)(2,1)}, u32[]{:S(2)}) copy-start(bf16[1024,1024]{1,0:T(8,128)(2,1)} %w_ref.3) | copy-start | bytes 6291460
  72.7 0.8 copy-start.1
  77.2 1.0 %copy-start.2 = (bf16[8,256,128]{2,1,0:T(8,128)(2,1)S(1)}, bf16[8,256,128]{2,1,0:T(8,128)(2,1)}, u32[]{:S(2)}) copy-start(bf16[8,256,128]{2,1,0:T(8,128)(2,1)} %copy-done.1) | copy-start | bytes 1572868

commit v3 on v2

--- a/solution.py
+++ b/solution.py
@@ -29,21 +29,22 @@
 
 
 def first_move(steps, count, head):
-    def move(tokens, cache, w_uvqk):
+    def move(tokens, cache):
         if steps == 0:
-            split, w_query, moved = prepare(cache, w_uvqk, head, tokens)
-            return moved, split, w_query
+            split, moved = prepare(cache, head, tokens)
+            return moved, split
         moved = rotate(tokens, steps, count)
-        split, w_query = prepare(cache, w_uvqk, head)
-        return moved, split, w_query
+        (split,) = prepare(cache, head)
+        return moved, split
 
     return move
 
 
 def second_move(steps, count, head):
-    def move(tokens, split, w_query):
+    def move(tokens, split, w_uvqk):
         moved = rotate(tokens, steps, count)
         cache = exchange(split)
+        w_query = fetch(w_uvqk)
         kept, query = project_query(moved, w_query, head)
         return kept, cache, query
 
@@ -86,18 +87,17 @@
     return pltpu.CompilerParams(vmem_limit_bytes=mebibytes << 20)
 
 
-def prepare(cache, w_uvqk, head, tokens=None):
+def prepare(cache, head, tokens=None):
     two, length, width = cache.shape
     heads = width // head
     shape = (heads, two, length, head)
     far = pl.BlockSpec(memory_space=pltpu.HBM)
-    near = pl.BlockSpec(memory_space=pltpu.VMEM)
 
     def kernel(*refs):
         if tokens is None:
-            cache_ref, w_ref, split_ref, query_ref, buf, reads, writes, sem = refs
+            cache_ref, split_ref, buf, reads, writes = refs
         else:
-            cache_ref, w_ref, tokens_ref, split_ref, query_ref, kept_ref, buf, reads, writes, sem, held, moves = refs
+            cache_ref, tokens_ref, split_ref, kept_ref, buf, reads, writes, held, moves = refs
             pull_tokens = pltpu.make_async_copy(tokens_ref, held, moves.at[0])
             push_tokens = pltpu.make_async_copy(held, kept_ref, moves.at[1])
 
@@ -119,28 +119,24 @@
             pull(h).wait()
             push(h).start()
 
-        weights = pltpu.make_async_copy(w_ref.at[:, 2 * width : 3 * width], query_ref, sem)
         if tokens is not None:
             pull_tokens.start()
         each(lambda h: pull(h).start())
-        weights.start()
         if tokens is not None:
             pull_tokens.wait()
             push_tokens.start()
         each(pass_on)
         each(lambda h: push(h).wait())
-        weights.wait()
         if tokens is not None:
             push_tokens.wait()
 
-    operands = [cache, w_uvqk]
-    out_specs = [far, near]
-    out_shape = [pltpu.HBM(shape, cache.dtype), pltpu.VMEM((width, width), w_uvqk.dtype)]
+    operands = [cache]
+    out_specs = [far]
+    out_shape = [pltpu.HBM(shape, cache.dtype)]
     scratch = [
         pltpu.VMEM(shape, cache.dtype),
         pltpu.SemaphoreType.DMA((heads,)),
         pltpu.SemaphoreType.DMA((heads,)),
-        pltpu.SemaphoreType.DMA,
     ]
     if tokens is not None:
         operands.append(tokens)
@@ -156,6 +152,26 @@
         compiler_params=limit(4),
         name="prepare",
     )(*operands)
+
+
+def fetch_kernel(w_uvqk_ref, query_ref, sem):
+    width = query_ref.shape[1]
+    copy = pltpu.make_async_copy(w_uvqk_ref.at[:, 2 * width : 3 * width], query_ref, sem)
+    copy.start()
+    copy.wait()
+
+
+def fetch(w_uvqk):
+    width = w_uvqk.shape[0]
+    return pl.pallas_call(
+        fetch_kernel,
+        in_specs=[pl.BlockSpec(memory_space=pltpu.HBM)],
+        out_specs=pl.BlockSpec(memory_space=pltpu.VMEM),
+        out_shape=pltpu.VMEM((width, width), w_uvqk.dtype),
+        scratch_shapes=[pltpu.SemaphoreType.DMA],
+        compiler_params=limit(1),
+        name="fetch",
+    )(w_uvqk)
 
 
 def query_kernel(tokens_ref, w_ref, kept_ref, out_ref, sem):
@@ -410,8 +426,8 @@
     second_moves = [second_move(by, groups, head) for by in seconds]
     w_uvqk = pltpu.with_memory_space_constraint(w_uvqk, pltpu.HBM)
     prefix = pltpu.with_memory_space_constraint(prefix_cache[0], pltpu.HBM)
-    tokens, split, w_query = lax.switch(first, first_moves, candidates[0], prefix, w_uvqk)
-    tokens, cache, query = lax.switch(second, second_moves, tokens, split, w_query)
+    tokens, split = lax.switch(first, first_moves, candidates[0], prefix)
+    tokens, cache, query = lax.switch(second, second_moves, tokens, split, w_uvqk)
     user = (group_here - offset) % groups
     table = jnp.stack([counts, prefix_len, jnp.full_like(counts, helper_here)])
     places = lax.broadcasted_iota(jnp.int32, table.shape, 1)

time: 81.1 us -> 80.7 us (level)
  waiting for transfers between devices: 36.6 us -> 35 us
  Pallas kernels: 23 us -> 24.2 us
    ppermute x1, waiting for transfers between devices: 25.2 us -> 23.6 us  [rotate(): return lax.ppermute(value, 'group', pairs)]
    pallas_call x0 -> x1, Pallas kernels: none -> 1.6 us  [fetch(): pl.pallas_call(fetch_kernel, in_specs=[pl.BlockSpec(memory_space=pltpu.HB...]
  transfers between devices with their start and end apart: 4 -> 4, of which waited for: 3 -> 3; matrix products, arithmetic and copies ran while one was open for 0% -> 0% of each run, Pallas kernels for 12% -> 14%
where the time goes in v3:
time: 80.7 us; the launch traced here: 80.3 us
  waiting for transfers between devices  35 us (43%)
  Pallas kernels  24.2 us (30%)
  starting transfers between devices  17.7 us (22%)
  local copies, waits for them, and re-layouts  1.93 us (2%)
  between operations  0.99 us (1%)
    ppermute x1, waiting for transfers between devices, rotate(): return lax.ppermute(value, 'group', pairs)  23.6 us
    all_to_all x3, starting transfers between devices, exchange(): return lax.all_to_all(value, 'helper', 0, 0, tiled=True)  14.5 us
    all_to_all x3, waiting for transfers between devices, exchange(): return lax.all_to_all(value, 'helper', 0, 0, tiled=True)  11.4 us
    pallas_call x1, Pallas kernels, attend(): pl.pallas_call(functools.partial(attend_kernel, head ** (-0.5), rows), in...  8.32 us
    pallas_call x1, Pallas kernels, project_own(): pl.pallas_call(functools.partial(own_kernel, head ** (-0.5), pieces), in_...  5.62 us
    ppermute x1, starting transfers between devices, rotate(): return lax.ppermute(value, 'group', pairs)  3.27 us
    pallas_call x1, Pallas kernels, prepare(): pl.pallas_call(kernel, in_specs=[far] * len(operands), out_specs=out_spec...  2.57 us
    pallas_call x1, Pallas kernels, finish(): pl.pallas_call(functools.partial(finish_kernel, pieces), in_specs=[pl.Blo...  2.29 us
  transfers between devices with their start and end apart: 4, of which 3 were waited for; matrix products, arithmetic and copies ran while one was open for 0% of the time, Pallas kernels for 14%

profile of v3, /device:TPU:32, one launch (start us, length us, event | category | flops | bytes accessed | tf_op | source)
XLA Modules:
  0.0 80.3 jit_solution(10920216237207095245)
XLA Ops:
  0.7 2.6 %conditional.2 = (bf16[256,1024]{1,0:T(8,128)(2,1)}, bf16[8,2,384,128]{3,2,1,0:T(8,128)(2,1)}) conditional(s32[]{:T(128)} %clamp.7, (bf16[256,1024]{1,0:T(8,128)(2,1)}, bf16[2,384,1024]{2,1,0:T(8,128)(2,1)}) %tuple.123, (bf16[256,1024]{1,0:T(8,128)(2,1)}, bf16[2,384,1024]{2,1,0:T(8,128)(2,1)}) %tuple.124, ...), branch_computations={%region_1.2_spmd, %region_2.3_spmd, %region_3.4_spmd, %region_4.5_... | conditional | bytes 2097208 | solution.py:429
  0.7 2.6 %prepare.13 = (bf16[8,2,384,128]{3,2,1,0:T(8,128)(2,1)}, bf16[256,1024]{1,0:T(8,128)(2,1)}) custom-call(bf16[2,384,1024]{2,1,0:T(8,128)(2,1)} %get-tuple-element.121.refs_0_, bf16[256,1024]{1,0:T(8,128)(2,1)} %get-tuple-element.122.refs_1_), custom_call_target="tpu_custom_call" | custom-call | tf_op jit(solution)/shard_map/cond/branch_4_fun/prepare/pallas_call | solution.py:146
  3.3 0.0 copy-start.4
  3.4 0.0 copy-start.5
  3.4 35.9 %conditional.3 = (bf16[256,1024]{1,0:T(8,128)(2,1)}, bf16[8,2,384,128]{3,2,1,0:T(8,128)(2,1)}, bf16[8,256,128]{2,1,0:T(8,128)(2,1)}) conditional(s32[]{:T(128)} %clamp.6, (bf16[256,1024]{1,0:T(8,128)(2,1)}, bf16[1024,4096]{1,0:T(8,128)(2,1)}, bf16[8,2,384,128]{3,2,1,0:T(8,128)(2,1)}) %tuple.91, ...), branch_computations={%region_10.11_spmd, %region_11.12_spmd, %region_12.13_spmd, %regio... | conditional | flops 536870912 | bytes 8912992 | solution.py:430
  3.6 5.3 %all-to-all-start.10 = ((bf16[8,2,384,128]{3,2,1,0:T(8,128)(2,1)}), bf16[8,2,384,128]{3,2,1,0:T(8,128)(2,1)}, u32[]{:S(2)}, u32[]{:S(2)}) async-start(bf16[8,2,384,128]{3,2,1,0:T(8,128)(2,1)} %get-tuple-element.186), calls=%async_computation.10 | async-start | bytes 3145728 | tf_op jit(solution)/shard_map/cond/branch_10_fun/all_to_all | solution.py:21
  8.9 3.3 %collective-permute-start.17 = (bf16[256,1024]{1,0:T(8,128)(2,1)}, bf16[256,1024]{1,0:T(8,128)(2,1)S(1)}, u32[]{:S(2)}, u32[]{:S(2)}) collective-permute-start(bf16[256,1024]{1,0:T(8,128)(2,1)} %get-tuple-element.183), channel_id=1, source_target_pairs={{0,64},{8,72},{16,80},{24,88},{32,96},{40,104},{48,112},{56,120},{... | collective-permute-start | bytes 1572872 | tf_op jit(solution)/shard_map/cond/branch_10_fun/ppermute | solution.py:28
  12.2 1.6 %fetch.22.w_ref = bf16[1024,1024]{1,0:T(8,128)(2,1)S(1)} custom-call(bf16[1024,4096]{1,0:T(8,128)(2,1)} %get-tuple-element.184.w_uvqk_ref), custom_call_target="tpu_custom_call" | custom-call | tf_op jit(solution)/shard_map/cond/branch_10_fun/fetch/pallas_call | solution.py:166
  13.8 23.6 %collective-permute-done.17.tokens_ref = bf16[256,1024]{1,0:T(8,128)(2,1)S(1)} collective-permute-done((bf16[256,1024]{1,0:T(8,128)(2,1)}, bf16[256,1024]{1,0:T(8,128)(2,1)S(1)}, u32[]{:S(2)}, u32[]{:S(2)}) %collective-permute-start.17) | collective-permute-done | bytes 524320 | tf_op jit(solution)/shard_map/cond/branch_10_fun/ppermute | solution.py:28
  37.4 1.8 %project_query.22 = (bf16[256,1024]{1,0:T(8,128)(2,1)}, bf16[8,256,128]{2,1,0:T(8,128)(2,1)}) custom-call(bf16[256,1024]{1,0:T(8,128)(2,1)S(1)} %collective-permute-done.17.tokens_ref, bf16[1024,1024]{1,0:T(8,128)(2,1)S(1)} %fetch.22.w_ref), custom_call_target="tpu_custom_call" | custom-call | flops 536870912 | bytes 2097152 | tf_op jit(solution)/shard_map/cond/branch_10_fun/project_query/pallas_call | solution.py:200
  39.3 0.0 all-to-all-done.10
  39.3 5.4 %all-to-all-start.12 = ((bf16[8,256,128]{2,1,0:T(8,128)(2,1)}), bf16[8,256,128]{2,1,0:T(8,128)(2,1)S(1)}, u32[]{:S(2)}, u32[]{:S(2)}) async-start(bf16[8,256,128]{2,1,0:T(8,128)(2,1)} %get-tuple-element.204.query_ref), calls=%async_computation.12 | async-start | bytes 1048576 | tf_op jit(solution)/shard_map/all_to_all | solution.py:21
  44.7 0.1 pad.2.clone
  44.8 0.0 copy-done.4
  44.8 0.0 copy-done.5
  44.8 0.2 fusion.meta_ref
  45.0 1.9 %visible_prefix.1 = (bf16[8,384,128]{2,1,0:T(8,128)(2,1)S(1)}, bf16[8,384,128]{2,1,0:T(8,128)(2,1)S(1)}) custom-call(s32[3]{0:T(128)S(1)} %fusion.meta_ref, bf16[8,2,384,128]{3,2,1,0:T(8,128)(2,1)} %get-tuple-element.205.cache_ref), custom_call_target="tpu_custom_call" | custom-call | tf_op jit(solution)/shard_map/visible_prefix/pallas_call | solution.py:303
  46.9 7.6 %all-to-all-done.12.query_ref = bf16[8,256,128]{2,1,0:T(8,128)(2,1)S(1)} async-done(((bf16[8,256,128]{2,1,0:T(8,128)(2,1)}), bf16[8,256,128]{2,1,0:T(8,128)(2,1)S(1)}, u32[]{:S(2)}, u32[]{:S(2)}) %all-to-all-start.12) | async-done | bytes 524320 | tf_op jit(solution)/shard_map/all_to_all | solution.py:21
  54.5 0.0 copy-start.3
  54.5 8.3 %attend.1 = bf16[8,256,128]{2,1,0:T(8,128)(2,1)} custom-call(s32[3]{0:T(128)S(1)} %fusion.meta_ref, bf16[8,256,128]{2,1,0:T(8,128)(2,1)S(1)} %all-to-all-done.12.query_ref, bf16[8,384,128]{2,1,0:T(8,128)(2,1)S(1)} %get-tuple-element.206.keys_ref, bf16[8,384,128]{2,1,0:T(8,128)(2,1)S(1)} %get-tuple-element.207.values_ref), custom_call_target="tpu_custom_call" | custom-call | flops 3221225472 | bytes 1572864 | tf_op jit(solution)/shard_map/attend/pallas_call | solution.py:356
  62.9 3.7 %all-to-all-start.13 = ((bf16[8,256,128]{2,1,0:T(8,128)(2,1)}), bf16[8,256,128]{2,1,0:T(8,128)(2,1)S(1)}, u32[]{:S(2)}, u32[]{:S(2)}) async-start(bf16[8,256,128]{2,1,0:T(8,128)(2,1)} %attend.1), calls=%async_computation.13 | async-start | bytes 1048576 | tf_op jit(solution)/shard_map/all_to_all | solution.py:21
  66.6 0.0 copy-done.3
  66.6 0.0 copy-start
  66.6 5.6 %project_own.1 = (bf16[256,1024]{1,0:T(8,128)(2,1)S(1)}, bf16[8,256,128]{2,1,0:T(8,128)(2,1)S(1)}) custom-call(bf16[256,1024]{1,0:T(8,128)(2,1)} %get-tuple-element.208.tokens_ref, bf16[8,256,128]{2,1,0:T(8,128)(2,1)} %get-tuple-element.204.query_ref, f32[1,1024]{1,0:T(1,128)S(1)} %bitcast.9, bf16[1024,4096]{1,0:T(8,128)(2,1)} %w_ref.2), custom_call_target="tpu_custom_call" | custom-call | flops 1610612736 | bytes 6291456 | tf_op jit(solution)/shard_map/project_own/pallas_call | solution.py:261
  72.2 0.0 copy-start.1
  72.2 0.8 copy-done.1
  73.0 3.7 %all-to-all-done.13.mixed_ref = bf16[8,256,128]{2,1,0:T(8,128)(2,1)S(1)} async-done(((bf16[8,256,128]{2,1,0:T(8,128)(2,1)}), bf16[8,256,128]{2,1,0:T(8,128)(2,1)S(1)}, u32[]{:S(2)}, u32[]{:S(2)}) %all-to-all-start.13) | async-done | bytes 524320 | tf_op jit(solution)/shard_map/all_to_all | solution.py:21
  76.8 0.0 copy-done
  76.8 0.0 copy-start.2
  76.8 1.0 %copy-done.2 = bf16[8,256,128]{2,1,0:T(8,128)(2,1)S(1)} copy-done((bf16[8,256,128]{2,1,0:T(8,128)(2,1)S(1)}, bf16[8,256,128]{2,1,0:T(8,128)(2,1)}, u32[]{:S(2)}) %copy-start.2) | copy-done | bytes 524312
  77.8 2.3 %finish.1 = bf16[256,1024]{1,0:T(8,128)(2,1)} custom-call(s32[3]{0:T(128)S(1)} %fusion.meta_ref, bf16[8,256,128]{2,1,0:T(8,128)(2,1)S(1)} %all-to-all-done.13.mixed_ref, bf16[8,256,128]{2,1,0:T(8,128)(2,1)S(1)} %copy-done.2, bf16[256,1024]{1,0:T(8,128)(2,1)S(1)} %get-tuple-element.210.gate_ref, bf16[1024,1024]{1,0:T(8,128)(2,1)S(1)} %copy-done), custom_call_target="tpu_custom_call" | custom-call | flops 536870912 | bytes 2097152 | tf_op jit(solution)/shard_map/finish/pallas_call | solution.py:401
  (1 shorter events, 0.0 us)
Async XLA Ops:
  3.3 41.4 %copy-start.4 = (s32[32]{0:T(128)S(1)}, s32[32]{0:T(128)}, u32[]{:S(2)}) copy-start(s32[32]{0:T(128)} %param.36) | copy-start | bytes 388
  3.4 41.4 %copy-start.5 = (s32[32]{0:T(128)S(1)}, s32[32]{0:T(128)}, u32[]{:S(2)}) copy-start(s32[32]{0:T(128)} %param.35) | copy-start | bytes 388
  3.6 35.7 %all-to-all-start.10 = ((bf16[8,2,384,128]{3,2,1,0:T(8,128)(2,1)}), bf16[8,2,384,128]{3,2,1,0:T(8,128)(2,1)}, u32[]{:S(2)}, u32[]{:S(2)}) async-start(bf16[8,2,384,128]{3,2,1,0:T(8,128)(2,1)} %get-tuple-element.186), calls=%async_computation.10 | async-start | bytes 3145728 | tf_op jit(solution)/shard_map/cond/branch_10_fun/all_to_all | solution.py:21
  8.9 28.5 %collective-permute-start.17 = (bf16[256,1024]{1,0:T(8,128)(2,1)}, bf16[256,1024]{1,0:T(8,128)(2,1)S(1)}, u32[]{:S(2)}, u32[]{:S(2)}) collective-permute-start(bf16[256,1024]{1,0:T(8,128)(2,1)} %get-tuple-element.183), channel_id=1, source_target_pairs={{0,64},{8,72},{16,80},{24,88},{32,96},{40,104},{48,112},{56,120},{... | collective-permute-start | bytes 1572872 | tf_op jit(solution)/shard_map/cond/branch_10_fun/ppermute | solution.py:28
  39.3 15.3 %all-to-all-start.12 = ((bf16[8,256,128]{2,1,0:T(8,128)(2,1)}), bf16[8,256,128]{2,1,0:T(8,128)(2,1)S(1)}, u32[]{:S(2)}, u32[]{:S(2)}) async-start(bf16[8,256,128]{2,1,0:T(8,128)(2,1)} %get-tuple-element.204.query_ref), calls=%async_computation.12 | async-start | bytes 1048576 | tf_op jit(solution)/shard_map/all_to_all | solution.py:21
  54.5 12.0 %copy-start.3 = (f32[1024]{0:T(1024)S(1)}, f32[1024]{0:T(1024)}, u32[]{:S(2)}) copy-start(f32[1024]{0:T(1024)} %param.33) | copy-start | bytes 12292
  62.9 13.9 %all-to-all-start.13 = ((bf16[8,256,128]{2,1,0:T(8,128)(2,1)}), bf16[8,256,128]{2,1,0:T(8,128)(2,1)S(1)}, u32[]{:S(2)}, u32[]{:S(2)}) async-start(bf16[8,256,128]{2,1,0:T(8,128)(2,1)} %attend.1), calls=%async_computation.13 | async-start | bytes 1048576 | tf_op jit(solution)/shard_map/all_to_all | solution.py:21
  66.6 10.2 %copy-start = (bf16[1024,1024]{1,0:T(8,128)(2,1)S(1)}, bf16[1024,1024]{1,0:T(8,128)(2,1)}, u32[]{:S(2)}) copy-start(bf16[1024,1024]{1,0:T(8,128)(2,1)} %w_ref.3) | copy-start | bytes 6291460
  72.2 0.8 copy-start.1
  76.8 1.0 %copy-start.2 = (bf16[8,256,128]{2,1,0:T(8,128)(2,1)S(1)}, bf16[8,256,128]{2,1,0:T(8,128)(2,1)}, u32[]{:S(2)}) copy-start(bf16[8,256,128]{2,1,0:T(8,128)(2,1)} %copy-done.1) | copy-start | bytes 1572868

commit v4 on v3

--- a/solution.py
+++ b/solution.py
@@ -311,11 +311,10 @@
     )(meta, cache)
 
 
-def attend_kernel(scale, rows, meta_ref, query_ref, keys_ref, values_ref, out_ref):
+def attend_kernel(scale, rows, query_ref, keys_ref, values_ref, out_ref):
     blocks, slots, head = query_ref.shape
-    shards, _, _ = keys_ref.shape
+    shards = keys_ref.shape[0]
     per = rows // slots
-    live_blocks = jnp.minimum((meta_ref[0] + rows - 1) // rows, blocks // per)
 
     def row_block(number, carry):
         first = number * per
@@ -338,16 +337,10 @@
         out_ref[pl.ds(first, per)] = acc.astype(jnp.bfloat16).reshape(per, slots, head)
         return carry
 
-    lax.fori_loop(0, live_blocks, row_block, 0)
-
-    def dead_block(number, carry):
-        out_ref[pl.ds(number * per, per)] = jnp.zeros((per, slots, head), jnp.bfloat16)
-        return carry
-
-    lax.fori_loop(live_blocks, blocks // per, dead_block, 0)
-
-
-def attend(meta, query, keys, values):
+    lax.fori_loop(0, blocks // per, row_block, 0)
+
+
+def attend(query, keys, values):
     blocks, slots, head = query.shape
     shards, length, _ = keys.shape
     rows = 4 * slots
@@ -355,7 +348,7 @@
     whole = pl.BlockSpec(memory_space=pltpu.VMEM)
     return pl.pallas_call(
         functools.partial(attend_kernel, head ** (-0.5), rows),
-        in_specs=[pl.BlockSpec(memory_space=pltpu.SMEM), whole, whole, whole],
+        in_specs=[whole, whole, whole],
         out_specs=whole,
         out_shape=jax.ShapeDtypeStruct(query.shape, jnp.bfloat16),
         cost_estimate=pl.CostEstimate(
@@ -363,13 +356,13 @@
         ),
         compiler_params=limit(14),
         name="attend",
-    )(meta, query, keys, values)
-
-
-def finish_kernel(pieces, meta_ref, mixed_ref, own_ref, gate_ref, w_ref, out_ref, buf, sems):
+    )(query, keys, values)
+
+
+def finish_kernel(pieces, facts_ref, mixed_ref, own_ref, gate_ref, w_ref, out_ref, buf, meta_ref, sems, sem):
     heads, slots, head = mixed_ref.shape
-    count = meta_ref[0]
-    first = meta_ref[2] * slots
+    facts = pltpu.make_async_copy(facts_ref, meta_ref, sem)
+    facts.start()
     width = heads * head
     rows = slots // pieces
     copies = []
@@ -386,6 +379,10 @@
         spread = jnp.sum(centre * centre, axis=-1, keepdims=True) * (1.0 / width)
         normed = centre * lax.rsqrt(spread + 1e-05) * gate_ref[here].astype(jnp.float32)
         result = jnp.dot(normed.astype(jnp.bfloat16), w_ref[...], preferred_element_type=jnp.float32)
+        if piece == 0:
+            facts.wait()
+            count = meta_ref[0]
+            first = meta_ref[2] * slots
         place = first + piece * rows + lax.broadcasted_iota(jnp.int32, result.shape, 0)
         buf[here] = jnp.where(place < count, result, 0.0).astype(jnp.bfloat16)
         copies.append(pltpu.make_async_copy(buf.at[here], out_ref.at[here], sems.at[piece]))
@@ -400,9 +397,14 @@
     whole = pl.BlockSpec(memory_space=pltpu.VMEM)
     return pl.pallas_call(
         functools.partial(finish_kernel, pieces),
-        in_specs=[pl.BlockSpec(memory_space=pltpu.SMEM)] + [whole] * 4,
+        in_specs=[pl.BlockSpec(memory_space=pl.ANY)] + [whole] * 4,
         out_specs=pl.BlockSpec(memory_space=pltpu.HBM),
-        scratch_shapes=[pltpu.VMEM((slots, width), jnp.bfloat16), pltpu.SemaphoreType.DMA((pieces,))],
+        scratch_shapes=[
+            pltpu.VMEM((slots, width), jnp.bfloat16),
+            pltpu.SMEM(meta.shape, meta.dtype),
+            pltpu.SemaphoreType.DMA((pieces,)),
+            pltpu.SemaphoreType.DMA,
+        ],
         out_shape=jax.ShapeDtypeStruct((slots, width), jnp.bfloat16),
         cost_estimate=pl.CostEstimate(
             flops=2 * slots * width * width, bytes_accessed=2 * width * width, transcendentals=slots
@@ -435,7 +437,7 @@
     query_all = exchange(query)
     gate, own = project_own(tokens, query, norm_gain, w_uvqk, head)
     keys, values = visible_prefix(meta, cache)
-    heads_out = attend(meta, query_all, keys, values)
+    heads_out = attend(query_all, keys, values)
     mixed = exchange(heads_out)
     return finish(meta, mixed, own, gate, w_output)[None]
 

time: 80.7 us -> 79.9 us (0.990)
  no operation moved by 1% of the time
where the time goes in v4:
time: 79.9 us; the launch traced here: 79.5 us
  waiting for transfers between devices  35 us (44%)
  Pallas kernels  23.4 us (29%)
  starting transfers between devices  17.7 us (22%)
  local copies, waits for them, and re-layouts  1.93 us (2%)
  between operations  0.99 us (1%)
    ppermute x1, waiting for transfers between devices, rotate(): return lax.ppermute(value, 'group', pairs)  23.6 us
    all_to_all x3, starting transfers between devices, exchange(): return lax.all_to_all(value, 'helper', 0, 0, tiled=True)  14.5 us
    all_to_all x3, waiting for transfers between devices, exchange(): return lax.all_to_all(value, 'helper', 0, 0, tiled=True)  11.4 us
    pallas_call x1, Pallas kernels, attend(): pl.pallas_call(functools.partial(attend_kernel, head ** (-0.5), rows), in...  7.76 us
    pallas_call x1, Pallas kernels, project_own(): pl.pallas_call(functools.partial(own_kernel, head ** (-0.5), pieces), in_...  5.62 us
    ppermute x1, starting transfers between devices, rotate(): return lax.ppermute(value, 'group', pairs)  3.27 us
    pallas_call x1, Pallas kernels, prepare(): pl.pallas_call(kernel, in_specs=[far] * len(operands), out_specs=out_spec...  2.57 us
    pallas_call x1, Pallas kernels, finish(): pl.pallas_call(functools.partial(finish_kernel, pieces), in_specs=[pl.Blo...  2.06 us
  transfers between devices with their start and end apart: 4, of which 3 were waited for; matrix products, arithmetic and copies ran while one was open for 0% of the time, Pallas kernels for 14%

profile of v4, /device:TPU:32, one launch (start us, length us, event | category | flops | bytes accessed | tf_op | source)
XLA Modules:
  0.0 79.5 jit_solution(10916359321301818350)
XLA Ops:
  0.7 2.6 %conditional.2 = (bf16[256,1024]{1,0:T(8,128)(2,1)}, bf16[8,2,384,128]{3,2,1,0:T(8,128)(2,1)}) conditional(s32[]{:T(128)} %clamp.7, (bf16[256,1024]{1,0:T(8,128)(2,1)}, bf16[2,384,1024]{2,1,0:T(8,128)(2,1)}) %tuple.123, (bf16[256,1024]{1,0:T(8,128)(2,1)}, bf16[2,384,1024]{2,1,0:T(8,128)(2,1)}) %tuple.124, ...), branch_computations={%region_1.2_spmd, %region_2.3_spmd, %region_3.4_spmd, %region_4.5_... | conditional | bytes 2097208 | solution.py:431
  0.7 2.6 %prepare.13 = (bf16[8,2,384,128]{3,2,1,0:T(8,128)(2,1)}, bf16[256,1024]{1,0:T(8,128)(2,1)}) custom-call(bf16[2,384,1024]{2,1,0:T(8,128)(2,1)} %get-tuple-element.121.refs_0_, bf16[256,1024]{1,0:T(8,128)(2,1)} %get-tuple-element.122.refs_1_), custom_call_target="tpu_custom_call" | custom-call | tf_op jit(solution)/shard_map/cond/branch_4_fun/prepare/pallas_call | solution.py:146
  3.3 0.0 copy-start.4
  3.4 0.0 copy-start.5
  3.4 35.9 %conditional.3 = (bf16[256,1024]{1,0:T(8,128)(2,1)}, bf16[8,2,384,128]{3,2,1,0:T(8,128)(2,1)}, bf16[8,256,128]{2,1,0:T(8,128)(2,1)}) conditional(s32[]{:T(128)} %clamp.6, (bf16[256,1024]{1,0:T(8,128)(2,1)}, bf16[1024,4096]{1,0:T(8,128)(2,1)}, bf16[8,2,384,128]{3,2,1,0:T(8,128)(2,1)}) %tuple.91, ...), branch_computations={%region_10.11_spmd, %region_11.12_spmd, %region_12.13_spmd, %regio... | conditional | flops 536870912 | bytes 8912992 | solution.py:432
  3.6 5.3 %all-to-all-start.10 = ((bf16[8,2,384,128]{3,2,1,0:T(8,128)(2,1)}), bf16[8,2,384,128]{3,2,1,0:T(8,128)(2,1)}, u32[]{:S(2)}, u32[]{:S(2)}) async-start(bf16[8,2,384,128]{3,2,1,0:T(8,128)(2,1)} %get-tuple-element.186), calls=%async_computation.10 | async-start | bytes 3145728 | tf_op jit(solution)/shard_map/cond/branch_10_fun/all_to_all | solution.py:21
  8.9 3.3 %collective-permute-start.17 = (bf16[256,1024]{1,0:T(8,128)(2,1)}, bf16[256,1024]{1,0:T(8,128)(2,1)S(1)}, u32[]{:S(2)}, u32[]{:S(2)}) collective-permute-start(bf16[256,1024]{1,0:T(8,128)(2,1)} %get-tuple-element.183), channel_id=1, source_target_pairs={{0,64},{8,72},{16,80},{24,88},{32,96},{40,104},{48,112},{56,120},{... | collective-permute-start | bytes 1572872 | tf_op jit(solution)/shard_map/cond/branch_10_fun/ppermute | solution.py:28
  12.2 1.6 %fetch.22.w_ref = bf16[1024,1024]{1,0:T(8,128)(2,1)S(1)} custom-call(bf16[1024,4096]{1,0:T(8,128)(2,1)} %get-tuple-element.184.w_uvqk_ref), custom_call_target="tpu_custom_call" | custom-call | tf_op jit(solution)/shard_map/cond/branch_10_fun/fetch/pallas_call | solution.py:166
  13.8 23.6 %collective-permute-done.17.tokens_ref = bf16[256,1024]{1,0:T(8,128)(2,1)S(1)} collective-permute-done((bf16[256,1024]{1,0:T(8,128)(2,1)}, bf16[256,1024]{1,0:T(8,128)(2,1)S(1)}, u32[]{:S(2)}, u32[]{:S(2)}) %collective-permute-start.17) | collective-permute-done | bytes 524320 | tf_op jit(solution)/shard_map/cond/branch_10_fun/ppermute | solution.py:28
  37.4 1.8 %project_query.22 = (bf16[256,1024]{1,0:T(8,128)(2,1)}, bf16[8,256,128]{2,1,0:T(8,128)(2,1)}) custom-call(bf16[256,1024]{1,0:T(8,128)(2,1)S(1)} %collective-permute-done.17.tokens_ref, bf16[1024,1024]{1,0:T(8,128)(2,1)S(1)} %fetch.22.w_ref), custom_call_target="tpu_custom_call" | custom-call | flops 536870912 | bytes 2097152 | tf_op jit(solution)/shard_map/cond/branch_10_fun/project_query/pallas_call | solution.py:200
  39.3 0.0 all-to-all-done.10
  39.3 5.4 %all-to-all-start.12 = ((bf16[8,256,128]{2,1,0:T(8,128)(2,1)}), bf16[8,256,128]{2,1,0:T(8,128)(2,1)S(1)}, u32[]{:S(2)}, u32[]{:S(2)}) async-start(bf16[8,256,128]{2,1,0:T(8,128)(2,1)} %get-tuple-element.204.query_ref), calls=%async_computation.12 | async-start | bytes 1048576 | tf_op jit(solution)/shard_map/all_to_all | solution.py:21
  44.7 0.1 pad.2.clone
  44.8 0.0 copy-done.4
  44.8 0.0 copy-done.5
  44.8 0.2 fusion.meta_ref.facts_ref
  45.0 1.9 %visible_prefix.1 = (bf16[8,384,128]{2,1,0:T(8,128)(2,1)S(1)}, bf16[8,384,128]{2,1,0:T(8,128)(2,1)S(1)}) custom-call(s32[3]{0:T(128)S(1)} %fusion.meta_ref.facts_ref, bf16[8,2,384,128]{3,2,1,0:T(8,128)(2,1)} %get-tuple-element.205.cache_ref), custom_call_target="tpu_custom_call" | custom-call | tf_op jit(solution)/shard_map/visible_prefix/pallas_call | solution.py:303
  46.9 7.6 %all-to-all-done.12.query_ref = bf16[8,256,128]{2,1,0:T(8,128)(2,1)S(1)} async-done(((bf16[8,256,128]{2,1,0:T(8,128)(2,1)}), bf16[8,256,128]{2,1,0:T(8,128)(2,1)S(1)}, u32[]{:S(2)}, u32[]{:S(2)}) %all-to-all-start.12) | async-done | bytes 524320 | tf_op jit(solution)/shard_map/all_to_all | solution.py:21
  54.5 0.0 copy-start.3
  54.5 7.8 %attend.1 = bf16[8,256,128]{2,1,0:T(8,128)(2,1)} custom-call(bf16[8,256,128]{2,1,0:T(8,128)(2,1)S(1)} %all-to-all-done.12.query_ref, bf16[8,384,128]{2,1,0:T(8,128)(2,1)S(1)} %get-tuple-element.206.keys_ref, bf16[8,384,128]{2,1,0:T(8,128)(2,1)S(1)} %get-tuple-element.207.values_ref), custom_call_target="tpu_custom_call" | custom-call | flops 3221225472 | bytes 1572864 | tf_op jit(solution)/shard_map/attend/pallas_call | solution.py:349
  62.3 3.7 %all-to-all-start.13 = ((bf16[8,256,128]{2,1,0:T(8,128)(2,1)}), bf16[8,256,128]{2,1,0:T(8,128)(2,1)S(1)}, u32[]{:S(2)}, u32[]{:S(2)}) async-start(bf16[8,256,128]{2,1,0:T(8,128)(2,1)} %attend.1), calls=%async_computation.13 | async-start | bytes 1048576 | tf_op jit(solution)/shard_map/all_to_all | solution.py:21
  66.0 0.0 copy-done.3
  66.0 0.0 copy-start
  66.0 5.6 %project_own.1 = (bf16[256,1024]{1,0:T(8,128)(2,1)S(1)}, bf16[8,256,128]{2,1,0:T(8,128)(2,1)S(1)}) custom-call(bf16[256,1024]{1,0:T(8,128)(2,1)} %get-tuple-element.208.tokens_ref, bf16[8,256,128]{2,1,0:T(8,128)(2,1)} %get-tuple-element.204.query_ref, f32[1,1024]{1,0:T(1,128)S(1)} %bitcast.9, bf16[1024,4096]{1,0:T(8,128)(2,1)} %w_ref.2), custom_call_target="tpu_custom_call" | custom-call | flops 1610612736 | bytes 6291456 | tf_op jit(solution)/shard_map/project_own/pallas_call | solution.py:261
  71.7 0.0 copy-start.1
  71.7 0.8 copy-done.1
  72.5 3.7 %all-to-all-done.13.mixed_ref = bf16[8,256,128]{2,1,0:T(8,128)(2,1)S(1)} async-done(((bf16[8,256,128]{2,1,0:T(8,128)(2,1)}), bf16[8,256,128]{2,1,0:T(8,128)(2,1)S(1)}, u32[]{:S(2)}, u32[]{:S(2)}) %all-to-all-start.13) | async-done | bytes 524320 | tf_op jit(solution)/shard_map/all_to_all | solution.py:21
  76.2 0.0 copy-done
  76.2 0.0 copy-start.2
  76.2 1.0 %copy-done.2 = bf16[8,256,128]{2,1,0:T(8,128)(2,1)S(1)} copy-done((bf16[8,256,128]{2,1,0:T(8,128)(2,1)S(1)}, bf16[8,256,128]{2,1,0:T(8,128)(2,1)}, u32[]{:S(2)}) %copy-start.2) | copy-done | bytes 524312
  77.2 2.1 %finish.1 = bf16[256,1024]{1,0:T(8,128)(2,1)} custom-call(s32[3]{0:T(128)S(1)} %fusion.meta_ref.facts_ref, bf16[8,256,128]{2,1,0:T(8,128)(2,1)S(1)} %all-to-all-done.13.mixed_ref, bf16[8,256,128]{2,1,0:T(8,128)(2,1)S(1)} %copy-done.2, bf16[256,1024]{1,0:T(8,128)(2,1)S(1)} %get-tuple-element.210.gate_ref, bf16[1024,1024]{1,0:T(8,128)(2,1)S(1)} %copy-done), custom_call_target="tpu_custom_call" | custom-call | flops 536870912 | bytes 2097152 | tf_op jit(solution)/shard_map/finish/pallas_call | solution.py:398
  (1 shorter events, 0.0 us)
Async XLA Ops:
  3.3 41.4 %copy-start.4 = (s32[32]{0:T(128)S(1)}, s32[32]{0:T(128)}, u32[]{:S(2)}) copy-start(s32[32]{0:T(128)} %param.36) | copy-start | bytes 388
  3.4 41.4 %copy-start.5 = (s32[32]{0:T(128)S(1)}, s32[32]{0:T(128)}, u32[]{:S(2)}) copy-start(s32[32]{0:T(128)} %param.35) | copy-start | bytes 388
  3.6 35.7 %all-to-all-start.10 = ((bf16[8,2,384,128]{3,2,1,0:T(8,128)(2,1)}), bf16[8,2,384,128]{3,2,1,0:T(8,128)(2,1)}, u32[]{:S(2)}, u32[]{:S(2)}) async-start(bf16[8,2,384,128]{3,2,1,0:T(8,128)(2,1)} %get-tuple-element.186), calls=%async_computation.10 | async-start | bytes 3145728 | tf_op jit(solution)/shard_map/cond/branch_10_fun/all_to_all | solution.py:21
  8.9 28.5 %collective-permute-start.17 = (bf16[256,1024]{1,0:T(8,128)(2,1)}, bf16[256,1024]{1,0:T(8,128)(2,1)S(1)}, u32[]{:S(2)}, u32[]{:S(2)}) collective-permute-start(bf16[256,1024]{1,0:T(8,128)(2,1)} %get-tuple-element.183), channel_id=1, source_target_pairs={{0,64},{8,72},{16,80},{24,88},{32,96},{40,104},{48,112},{56,120},{... | collective-permute-start | bytes 1572872 | tf_op jit(solution)/shard_map/cond/branch_10_fun/ppermute | solution.py:28
  39.3 15.3 %all-to-all-start.12 = ((bf16[8,256,128]{2,1,0:T(8,128)(2,1)}), bf16[8,256,128]{2,1,0:T(8,128)(2,1)S(1)}, u32[]{:S(2)}, u32[]{:S(2)}) async-start(bf16[8,256,128]{2,1,0:T(8,128)(2,1)} %get-tuple-element.204.query_ref), calls=%async_computation.12 | async-start | bytes 1048576 | tf_op jit(solution)/shard_map/all_to_all | solution.py:21
  54.5 11.5 %copy-start.3 = (f32[1024]{0:T(1024)S(1)}, f32[1024]{0:T(1024)}, u32[]{:S(2)}) copy-start(f32[1024]{0:T(1024)} %param.33) | copy-start | bytes 12292
  62.3 13.9 %all-to-all-start.13 = ((bf16[8,256,128]{2,1,0:T(8,128)(2,1)}), bf16[8,256,128]{2,1,0:T(8,128)(2,1)S(1)}, u32[]{:S(2)}, u32[]{:S(2)}) async-start(bf16[8,256,128]{2,1,0:T(8,128)(2,1)} %attend.1), calls=%async_computation.13 | async-start | bytes 1048576 | tf_op jit(solution)/shard_map/all_to_all | solution.py:21
  66.0 10.2 %copy-start = (bf16[1024,1024]{1,0:T(8,128)(2,1)S(1)}, bf16[1024,1024]{1,0:T(8,128)(2,1)}, u32[]{:S(2)}) copy-start(bf16[1024,1024]{1,0:T(8,128)(2,1)} %w_ref.3) | copy-start | bytes 6291460
  71.7 0.8 %copy-start.1 = (bf16[8,256,128]{2,1,0:T(8,128)(2,1)}, bf16[8,256,128]{2,1,0:T(8,128)(2,1)S(1)}, u32[]{:S(2)}) copy-start(bf16[8,256,128]{2,1,0:T(8,128)(2,1)S(1)} %get-tuple-element.209.own_ref) | copy-start | bytes 1572868
  76.2 1.0 %copy-start.2 = (bf16[8,256,128]{2,1,0:T(8,128)(2,1)S(1)}, bf16[8,256,128]{2,1,0:T(8,128)(2,1)}, u32[]{:S(2)}) copy-start(bf16[8,256,128]{2,1,0:T(8,128)(2,1)} %copy-done.1) | copy-start | bytes 1572868

commit v5 on v4

--- a/solution.py
+++ b/solution.py
@@ -45,7 +45,8 @@
         moved = rotate(tokens, steps, count)
         cache = exchange(split)
         w_query = fetch(w_uvqk)
-        kept, query = project_query(moved, w_query, head)
+        parts = 1 if abs(steps) > FAR else 2
+        kept, query = project_query(moved, w_query, head, parts)
         return kept, cache, query
 
     return move
@@ -56,10 +57,10 @@
     for offset in range(groups):
         signed = (offset + groups // 2 - 1) % groups - groups // 2 + 1
         size, sign = abs(signed), 1 if signed > 0 else -1
-        if size < FAR:
+        if size <= 2:
             steps.append((0, signed))
             continue
-        far = groups // 2 if size >= groups // 2 - FAR else size // FAR * FAR
+        far = groups // 2 if size >= groups // 2 - FAR else (size + (size < FAR)) // FAR * FAR
         steps.append((sign * (size - far), sign * far if far < groups // 2 else far))
     firsts = sorted({first for first, _ in steps})
     seconds = sorted({second for _, second in steps})
@@ -174,31 +175,36 @@
     )(w_uvqk)
 
 
-def query_kernel(tokens_ref, w_ref, kept_ref, out_ref, sem):
+def query_kernel(parts, tokens_ref, w_ref, kept_ref, out_ref, sem):
     heads, _, head = out_ref.shape
     keep = pltpu.make_async_copy(tokens_ref, kept_ref, sem)
     keep.start()
     tokens = tokens_ref[...]
-    per = heads // 2
+    per = heads // parts
 
     def some_heads(part, carry):
-        cols = pl.ds(pl.multiple_of(part * per * head, head), per * head)
-        proj = jnp.dot(tokens, w_ref[:, cols], preferred_element_type=jnp.float32)
-        proj = silu(proj).astype(jnp.bfloat16)
-        for h in range(per):
-            out_ref[part * per + h] = proj[:, h * head : (h + 1) * head]
+        for h in range(0, per, 2):
+            first = (part * per + h) * head
+            cols = pl.ds(first if parts == 1 else pl.multiple_of(first, head), 2 * head)
+            proj = jnp.dot(tokens, w_ref[:, cols], preferred_element_type=jnp.float32)
+            proj = silu(proj).astype(jnp.bfloat16)
+            out_ref[part * per + h] = proj[:, :head]
+            out_ref[part * per + h + 1] = proj[:, head:]
         return carry
 
-    lax.fori_loop(0, 2, some_heads, 0)
+    if parts == 1:
+        some_heads(0, 0)
+    else:
+        lax.fori_loop(0, parts, some_heads, 0)
     keep.wait()
 
 
-def project_query(tokens, w_query, head):
+def project_query(tokens, w_query, head, parts):
     slots, width = tokens.shape
     heads = width // head
     whole = pl.BlockSpec(memory_space=pltpu.VMEM)
     return pl.pallas_call(
-        query_kernel,
+        functools.partial(query_kernel, parts),
         in_specs=[whole, whole],
         out_specs=[pl.BlockSpec(memory_space=pltpu.HBM), whole],
         out_shape=[
@@ -316,9 +322,8 @@
     shards = keys_ref.shape[0]
     per = rows // slots
 
-    def row_block(number, carry):
-        first = number * per
-        query = query_ref[pl.ds(first, per)].reshape(rows, head)
+    for first in range(0, blocks, per):
+        query = query_ref[first : first + per].reshape(rows, head)
         query = (query.astype(jnp.float32) * (0.5 * scale)).astype(jnp.bfloat16)
 
         def scores(shard):
@@ -334,10 +339,7 @@
                 ahead = scores(shard + 1)
             weight = half + half * jnp.tanh(half)
             acc = acc + jnp.dot(weight, values_ref[shard], preferred_element_type=jnp.float32)
-        out_ref[pl.ds(first, per)] = acc.astype(jnp.bfloat16).reshape(per, slots, head)
-        return carry
-
-    lax.fori_loop(0, blocks // per, row_block, 0)
+        out_ref[first : first + per] = acc.astype(jnp.bfloat16).reshape(per, slots, head)
 
 
 def attend(query, keys, values):

time: 79.9 us -> 79.3 us (level)
  no operation moved by 1% of the time
where the time goes in v5:
time: 79.3 us; the launch traced here: 78.9 us
  waiting for transfers between devices  34.9 us (44%)
  Pallas kernels  23.1 us (29%)
  starting transfers between devices  17.5 us (22%)
  local copies, waits for them, and re-layouts  1.93 us (2%)
  between operations  0.99 us (1%)
    ppermute x1, waiting for transfers between devices, rotate(): return lax.ppermute(value, 'group', pairs)  23.6 us
    all_to_all x3, starting transfers between devices, exchange(): return lax.all_to_all(value, 'helper', 0, 0, tiled=True)  14.3 us
    all_to_all x3, waiting for transfers between devices, exchange(): return lax.all_to_all(value, 'helper', 0, 0, tiled=True)  11.3 us
    pallas_call x1, Pallas kernels, attend(): pl.pallas_call(functools.partial(attend_kernel, head ** (-0.5), rows), in...  7.56 us
    pallas_call x1, Pallas kernels, project_own(): pl.pallas_call(functools.partial(own_kernel, head ** (-0.5), pieces), in_...  5.62 us
    ppermute x1, starting transfers between devices, rotate(): return lax.ppermute(value, 'group', pairs)  3.27 us
    pallas_call x1, Pallas kernels, prepare(): pl.pallas_call(kernel, in_specs=[far] * len(operands), out_specs=out_spec...  2.61 us
    pallas_call x1, Pallas kernels, finish(): pl.pallas_call(functools.partial(finish_kernel, pieces), in_specs=[pl.Blo...  2.06 us
  transfers between devices with their start and end apart: 4, of which 3 were waited for; matrix products, arithmetic and copies ran while one was open for 0% of the time, Pallas kernels for 14%

profile of v5, /device:TPU:32, one launch (start us, length us, event | category | flops | bytes accessed | tf_op | source)
XLA Modules:
  0.0 78.9 jit_solution(3967469910813691559)
XLA Ops:
  0.7 2.7 %conditional.2 = (bf16[256,1024]{1,0:T(8,128)(2,1)}, bf16[8,2,384,128]{3,2,1,0:T(8,128)(2,1)}) conditional(s32[]{:T(128)} %clamp.7, (bf16[256,1024]{1,0:T(8,128)(2,1)}, bf16[2,384,1024]{2,1,0:T(8,128)(2,1)}) %tuple.113, (bf16[256,1024]{1,0:T(8,128)(2,1)}, bf16[2,384,1024]{2,1,0:T(8,128)(2,1)}) %tuple.114, ...), branch_computations={%region_1.2_spmd, %region_2.3_spmd, %region_3.4_spmd, %region_4.5_... | conditional | bytes 2097208 | solution.py:433
  0.7 2.6 %prepare.13 = (bf16[8,2,384,128]{3,2,1,0:T(8,128)(2,1)}, bf16[256,1024]{1,0:T(8,128)(2,1)}) custom-call(bf16[2,384,1024]{2,1,0:T(8,128)(2,1)} %get-tuple-element.109.refs_0_, bf16[256,1024]{1,0:T(8,128)(2,1)} %get-tuple-element.110.refs_1_), custom_call_target="tpu_custom_call" | custom-call | tf_op jit(solution)/shard_map/cond/branch_4_fun/prepare/pallas_call | solution.py:147
  3.4 0.0 copy-start.4
  3.4 0.0 copy-start.5
  3.4 35.7 %conditional.3 = (bf16[256,1024]{1,0:T(8,128)(2,1)}, bf16[8,2,384,128]{3,2,1,0:T(8,128)(2,1)}, bf16[8,256,128]{2,1,0:T(8,128)(2,1)}) conditional(s32[]{:T(128)} %clamp.6, (bf16[256,1024]{1,0:T(8,128)(2,1)}, bf16[1024,4096]{1,0:T(8,128)(2,1)}, bf16[8,2,384,128]{3,2,1,0:T(8,128)(2,1)}) %tuple.83, ...), branch_computations={%region_10.11_spmd, %region_11.12_spmd, %region_12.13_spmd, %regio... | conditional | flops 536870912 | bytes 8912992 | solution.py:434
  3.6 5.3 %all-to-all-start.8 = ((bf16[8,2,384,128]{3,2,1,0:T(8,128)(2,1)}), bf16[8,2,384,128]{3,2,1,0:T(8,128)(2,1)}, u32[]{:S(2)}, u32[]{:S(2)}) async-start(bf16[8,2,384,128]{3,2,1,0:T(8,128)(2,1)} %get-tuple-element.164), calls=%async_computation.8 | async-start | bytes 3145728 | tf_op jit(solution)/shard_map/cond/branch_8_fun/all_to_all | solution.py:21
  9.0 3.3 %collective-permute-start.15 = (bf16[256,1024]{1,0:T(8,128)(2,1)}, bf16[256,1024]{1,0:T(8,128)(2,1)S(1)}, u32[]{:S(2)}, u32[]{:S(2)}) collective-permute-start(bf16[256,1024]{1,0:T(8,128)(2,1)} %get-tuple-element.161), channel_id=1, source_target_pairs={{0,64},{8,72},{16,80},{24,88},{32,96},{40,104},{48,112},{56,120},{... | collective-permute-start | bytes 1572872 | tf_op jit(solution)/shard_map/cond/branch_8_fun/ppermute | solution.py:28
  12.2 1.6 %fetch.18.w_ref = bf16[1024,1024]{1,0:T(8,128)(2,1)S(1)} custom-call(bf16[1024,4096]{1,0:T(8,128)(2,1)} %get-tuple-element.162.w_uvqk_ref), custom_call_target="tpu_custom_call" | custom-call | tf_op jit(solution)/shard_map/cond/branch_8_fun/fetch/pallas_call | solution.py:167
  13.8 23.6 %collective-permute-done.15.tokens_ref = bf16[256,1024]{1,0:T(8,128)(2,1)S(1)} collective-permute-done((bf16[256,1024]{1,0:T(8,128)(2,1)}, bf16[256,1024]{1,0:T(8,128)(2,1)S(1)}, u32[]{:S(2)}, u32[]{:S(2)}) %collective-permute-start.15) | collective-permute-done | bytes 524320 | tf_op jit(solution)/shard_map/cond/branch_8_fun/ppermute | solution.py:28
  37.5 1.6 %project_query.18 = (bf16[256,1024]{1,0:T(8,128)(2,1)}, bf16[8,256,128]{2,1,0:T(8,128)(2,1)}) custom-call(bf16[256,1024]{1,0:T(8,128)(2,1)S(1)} %collective-permute-done.15.tokens_ref, bf16[1024,1024]{1,0:T(8,128)(2,1)S(1)} %fetch.18.w_ref), custom_call_target="tpu_custom_call" | custom-call | flops 536870912 | bytes 2097152 | tf_op jit(solution)/shard_map/cond/branch_8_fun/project_query/pallas_call | solution.py:206
  39.1 0.0 all-to-all-done.8
  39.1 5.4 %all-to-all-start.10 = ((bf16[8,256,128]{2,1,0:T(8,128)(2,1)}), bf16[8,256,128]{2,1,0:T(8,128)(2,1)S(1)}, u32[]{:S(2)}, u32[]{:S(2)}) async-start(bf16[8,256,128]{2,1,0:T(8,128)(2,1)} %get-tuple-element.182.query_ref), calls=%async_computation.10 | async-start | bytes 1048576 | tf_op jit(solution)/shard_map/all_to_all | solution.py:21
  44.5 0.1 pad.2.clone
  44.6 0.0 copy-done.4
  44.6 0.0 copy-done.5
  44.6 0.2 fusion.meta_ref.facts_ref
  44.8 2.0 %visible_prefix.1 = (bf16[8,384,128]{2,1,0:T(8,128)(2,1)S(1)}, bf16[8,384,128]{2,1,0:T(8,128)(2,1)S(1)}) custom-call(s32[3]{0:T(128)S(1)} %fusion.meta_ref.facts_ref, bf16[8,2,384,128]{3,2,1,0:T(8,128)(2,1)} %get-tuple-element.183.cache_ref), custom_call_target="tpu_custom_call" | custom-call | tf_op jit(solution)/shard_map/visible_prefix/pallas_call | solution.py:309
  46.8 7.6 %all-to-all-done.10.query_ref = bf16[8,256,128]{2,1,0:T(8,128)(2,1)S(1)} async-done(((bf16[8,256,128]{2,1,0:T(8,128)(2,1)}), bf16[8,256,128]{2,1,0:T(8,128)(2,1)S(1)}, u32[]{:S(2)}, u32[]{:S(2)}) %all-to-all-start.10) | async-done | bytes 524320 | tf_op jit(solution)/shard_map/all_to_all | solution.py:21
  54.4 0.0 copy-start.3
  54.4 7.6 %attend.1 = bf16[8,256,128]{2,1,0:T(8,128)(2,1)} custom-call(bf16[8,256,128]{2,1,0:T(8,128)(2,1)S(1)} %all-to-all-done.10.query_ref, bf16[8,384,128]{2,1,0:T(8,128)(2,1)S(1)} %get-tuple-element.184.keys_ref, bf16[8,384,128]{2,1,0:T(8,128)(2,1)S(1)} %get-tuple-element.185.values_ref), custom_call_target="tpu_custom_call" | custom-call | flops 3221225472 | bytes 1572864 | tf_op jit(solution)/shard_map/attend/pallas_call | solution.py:351
  61.9 3.5 %all-to-all-start.11 = ((bf16[8,256,128]{2,1,0:T(8,128)(2,1)}), bf16[8,256,128]{2,1,0:T(8,128)(2,1)S(1)}, u32[]{:S(2)}, u32[]{:S(2)}) async-start(bf16[8,256,128]{2,1,0:T(8,128)(2,1)} %attend.1), calls=%async_computation.11 | async-start | bytes 1048576 | tf_op jit(solution)/shard_map/all_to_all | solution.py:21
  65.4 0.0 copy-done.3
  65.4 0.0 copy-start
  65.5 5.6 %project_own.1 = (bf16[256,1024]{1,0:T(8,128)(2,1)S(1)}, bf16[8,256,128]{2,1,0:T(8,128)(2,1)S(1)}) custom-call(bf16[256,1024]{1,0:T(8,128)(2,1)} %get-tuple-element.186.tokens_ref, bf16[8,256,128]{2,1,0:T(8,128)(2,1)} %get-tuple-element.182.query_ref, f32[1,1024]{1,0:T(1,128)S(1)} %bitcast.9, bf16[1024,4096]{1,0:T(8,128)(2,1)} %w_ref.2), custom_call_target="tpu_custom_call" | custom-call | flops 1610612736 | bytes 6291456 | tf_op jit(solution)/shard_map/project_own/pallas_call | solution.py:267
  71.1 0.0 copy-start.1
  71.1 0.8 copy-done.1
  71.9 3.7 %all-to-all-done.11.mixed_ref = bf16[8,256,128]{2,1,0:T(8,128)(2,1)S(1)} async-done(((bf16[8,256,128]{2,1,0:T(8,128)(2,1)}), bf16[8,256,128]{2,1,0:T(8,128)(2,1)S(1)}, u32[]{:S(2)}, u32[]{:S(2)}) %all-to-all-start.11) | async-done | bytes 524320 | tf_op jit(solution)/shard_map/all_to_all | solution.py:21
  75.6 0.0 copy-done
  75.6 0.0 copy-start.2
  75.6 1.0 %copy-done.2 = bf16[8,256,128]{2,1,0:T(8,128)(2,1)S(1)} copy-done((bf16[8,256,128]{2,1,0:T(8,128)(2,1)S(1)}, bf16[8,256,128]{2,1,0:T(8,128)(2,1)}, u32[]{:S(2)}) %copy-start.2) | copy-done | bytes 524312
  76.7 2.1 %finish.1 = bf16[256,1024]{1,0:T(8,128)(2,1)} custom-call(s32[3]{0:T(128)S(1)} %fusion.meta_ref.facts_ref, bf16[8,256,128]{2,1,0:T(8,128)(2,1)S(1)} %all-to-all-done.11.mixed_ref, bf16[8,256,128]{2,1,0:T(8,128)(2,1)S(1)} %copy-done.2, bf16[256,1024]{1,0:T(8,128)(2,1)S(1)} %get-tuple-element.188.gate_ref, bf16[1024,1024]{1,0:T(8,128)(2,1)S(1)} %copy-done), custom_call_target="tpu_custom_call" | custom-call | flops 536870912 | bytes 2097152 | tf_op jit(solution)/shard_map/finish/pallas_call | solution.py:400
  (1 shorter events, 0.0 us)
Async XLA Ops:
  3.4 41.2 %copy-start.4 = (s32[32]{0:T(128)S(1)}, s32[32]{0:T(128)}, u32[]{:S(2)}) copy-start(s32[32]{0:T(128)} %param.34) | copy-start | bytes 388
  3.4 41.2 %copy-start.5 = (s32[32]{0:T(128)S(1)}, s32[32]{0:T(128)}, u32[]{:S(2)}) copy-start(s32[32]{0:T(128)} %param.33) | copy-start | bytes 388
  3.6 35.5 %all-to-all-start.8 = ((bf16[8,2,384,128]{3,2,1,0:T(8,128)(2,1)}), bf16[8,2,384,128]{3,2,1,0:T(8,128)(2,1)}, u32[]{:S(2)}, u32[]{:S(2)}) async-start(bf16[8,2,384,128]{3,2,1,0:T(8,128)(2,1)} %get-tuple-element.164), calls=%async_computation.8 | async-start | bytes 3145728 | tf_op jit(solution)/shard_map/cond/branch_8_fun/all_to_all | solution.py:21
  9.0 28.5 %collective-permute-start.15 = (bf16[256,1024]{1,0:T(8,128)(2,1)}, bf16[256,1024]{1,0:T(8,128)(2,1)S(1)}, u32[]{:S(2)}, u32[]{:S(2)}) collective-permute-start(bf16[256,1024]{1,0:T(8,128)(2,1)} %get-tuple-element.161), channel_id=1, source_target_pairs={{0,64},{8,72},{16,80},{24,88},{32,96},{40,104},{48,112},{56,120},{... | collective-permute-start | bytes 1572872 | tf_op jit(solution)/shard_map/cond/branch_8_fun/ppermute | solution.py:28
  39.1 15.3 %all-to-all-start.10 = ((bf16[8,256,128]{2,1,0:T(8,128)(2,1)}), bf16[8,256,128]{2,1,0:T(8,128)(2,1)S(1)}, u32[]{:S(2)}, u32[]{:S(2)}) async-start(bf16[8,256,128]{2,1,0:T(8,128)(2,1)} %get-tuple-element.182.query_ref), calls=%async_computation.10 | async-start | bytes 1048576 | tf_op jit(solution)/shard_map/all_to_all | solution.py:21
  54.4 11.1 %copy-start.3 = (f32[1024]{0:T(1024)S(1)}, f32[1024]{0:T(1024)}, u32[]{:S(2)}) copy-start(f32[1024]{0:T(1024)} %param.31) | copy-start | bytes 12292
  61.9 13.7 %all-to-all-start.11 = ((bf16[8,256,128]{2,1,0:T(8,128)(2,1)}), bf16[8,256,128]{2,1,0:T(8,128)(2,1)S(1)}, u32[]{:S(2)}, u32[]{:S(2)}) async-start(bf16[8,256,128]{2,1,0:T(8,128)(2,1)} %attend.1), calls=%async_computation.11 | async-start | bytes 1048576 | tf_op jit(solution)/shard_map/all_to_all | solution.py:21
  65.4 10.2 %copy-start = (bf16[1024,1024]{1,0:T(8,128)(2,1)S(1)}, bf16[1024,1024]{1,0:T(8,128)(2,1)}, u32[]{:S(2)}) copy-start(bf16[1024,1024]{1,0:T(8,128)(2,1)} %w_ref.3) | copy-start | bytes 6291460
  71.1 0.8 %copy-start.1 = (bf16[8,256,128]{2,1,0:T(8,128)(2,1)}, bf16[8,256,128]{2,1,0:T(8,128)(2,1)S(1)}, u32[]{:S(2)}) copy-start(bf16[8,256,128]{2,1,0:T(8,128)(2,1)S(1)} %get-tuple-element.187.own_ref) | copy-start | bytes 1572868
  75.6 1.0 %copy-start.2 = (bf16[8,256,128]{2,1,0:T(8,128)(2,1)S(1)}, bf16[8,256,128]{2,1,0:T(8,128)(2,1)}, u32[]{:S(2)}) copy-start(bf16[8,256,128]{2,1,0:T(8,128)(2,1)} %copy-done.1) | copy-start | bytes 1572868

commit v6 on v5

--- a/solution.py
+++ b/solution.py
@@ -60,7 +60,7 @@
         if size <= 2:
             steps.append((0, signed))
             continue
-        far = groups // 2 if size >= groups // 2 - FAR else (size + (size < FAR)) // FAR * FAR
+        far = groups // 2 if size >= groups // 2 - FAR else (size + (size < 2 * FAR)) // FAR * FAR
         steps.append((sign * (size - far), sign * far if far < groups // 2 else far))
     firsts = sorted({first for first, _ in steps})
     seconds = sorted({second for _, second in steps})
@@ -334,10 +334,10 @@
         acc = jnp.zeros((rows, head), jnp.float32)
         ahead = scores(0)
         for shard in range(shards):
-            half = ahead.astype(jnp.bfloat16)
+            half = ahead
             if shard + 1 < shards:
                 ahead = scores(shard + 1)
-            weight = half + half * jnp.tanh(half)
+            weight = (half + half * jnp.tanh(half)).astype(jnp.bfloat16)
             acc = acc + jnp.dot(weight, values_ref[shard], preferred_element_type=jnp.float32)
         out_ref[first : first + per] = acc.astype(jnp.bfloat16).reshape(per, slots, head)
 

time: 79.3 us -> 79.5 us (level)
  no operation moved by 1% of the time
where the time goes in v6:
time: 79.5 us; the launch traced here: 79 us
  waiting for transfers between devices  34.9 us (44%)
  Pallas kernels  23.2 us (29%)
  starting transfers between devices  17.5 us (22%)
  local copies, waits for them, and re-layouts  1.93 us (2%)
  between operations  0.99 us (1%)
    ppermute x1, waiting for transfers between devices, rotate(): return lax.ppermute(value, 'group', pairs)  23.6 us
    all_to_all x3, starting transfers between devices, exchange(): return lax.all_to_all(value, 'helper', 0, 0, tiled=True)  14.3 us
    all_to_all x3, waiting for transfers between devices, exchange(): return lax.all_to_all(value, 'helper', 0, 0, tiled=True)  11.3 us
    pallas_call x1, Pallas kernels, attend(): pl.pallas_call(functools.partial(attend_kernel, head ** (-0.5), rows), in...  7.7 us
    pallas_call x1, Pallas kernels, project_own(): pl.pallas_call(functools.partial(own_kernel, head ** (-0.5), pieces), in_...  5.62 us
    ppermute x1, starting transfers between devices, rotate(): return lax.ppermute(value, 'group', pairs)  3.27 us
    pallas_call x1, Pallas kernels, prepare(): pl.pallas_call(kernel, in_specs=[far] * len(operands), out_specs=out_spec...  2.61 us
    pallas_call x1, Pallas kernels, finish(): pl.pallas_call(functools.partial(finish_kernel, pieces), in_specs=[pl.Blo...  2.06 us
  transfers between devices with their start and end apart: 4, of which 3 were waited for; matrix products, arithmetic and copies ran while one was open for 0% of the time, Pallas kernels for 14%

profile of v6, /device:TPU:32, one launch (start us, length us, event | category | flops | bytes accessed | tf_op | source)
XLA Modules:
  0.0 79.0 jit_solution(8108820082181499415)
XLA Ops:
  0.7 2.7 %conditional.2 = (bf16[256,1024]{1,0:T(8,128)(2,1)}, bf16[8,2,384,128]{3,2,1,0:T(8,128)(2,1)}) conditional(s32[]{:T(128)} %clamp.7, (bf16[256,1024]{1,0:T(8,128)(2,1)}, bf16[2,384,1024]{2,1,0:T(8,128)(2,1)}) %tuple.113, (bf16[256,1024]{1,0:T(8,128)(2,1)}, bf16[2,384,1024]{2,1,0:T(8,128)(2,1)}) %tuple.114, ...), branch_computations={%region_1.2_spmd, %region_2.3_spmd, %region_3.4_spmd, %region_4.5_... | conditional | bytes 2097208 | solution.py:433
  0.7 2.6 %prepare.13 = (bf16[8,2,384,128]{3,2,1,0:T(8,128)(2,1)}, bf16[256,1024]{1,0:T(8,128)(2,1)}) custom-call(bf16[2,384,1024]{2,1,0:T(8,128)(2,1)} %get-tuple-element.109.refs_0_, bf16[256,1024]{1,0:T(8,128)(2,1)} %get-tuple-element.110.refs_1_), custom_call_target="tpu_custom_call" | custom-call | tf_op jit(solution)/shard_map/cond/branch_4_fun/prepare/pallas_call | solution.py:147
  3.4 0.0 copy-start.4
  3.4 0.0 copy-start.5
  3.4 35.7 %conditional.3 = (bf16[256,1024]{1,0:T(8,128)(2,1)}, bf16[8,2,384,128]{3,2,1,0:T(8,128)(2,1)}, bf16[8,256,128]{2,1,0:T(8,128)(2,1)}) conditional(s32[]{:T(128)} %clamp.6, (bf16[256,1024]{1,0:T(8,128)(2,1)}, bf16[1024,4096]{1,0:T(8,128)(2,1)}, bf16[8,2,384,128]{3,2,1,0:T(8,128)(2,1)}) %tuple.83, ...), branch_computations={%region_10.11_spmd, %region_11.12_spmd, %region_12.13_spmd, %regio... | conditional | flops 536870912 | bytes 8912992 | solution.py:434
  3.6 5.3 %all-to-all-start.8 = ((bf16[8,2,384,128]{3,2,1,0:T(8,128)(2,1)}), bf16[8,2,384,128]{3,2,1,0:T(8,128)(2,1)}, u32[]{:S(2)}, u32[]{:S(2)}) async-start(bf16[8,2,384,128]{3,2,1,0:T(8,128)(2,1)} %get-tuple-element.164), calls=%async_computation.8 | async-start | bytes 3145728 | tf_op jit(solution)/shard_map/cond/branch_8_fun/all_to_all | solution.py:21
  9.0 3.3 %collective-permute-start.15 = (bf16[256,1024]{1,0:T(8,128)(2,1)}, bf16[256,1024]{1,0:T(8,128)(2,1)S(1)}, u32[]{:S(2)}, u32[]{:S(2)}) collective-permute-start(bf16[256,1024]{1,0:T(8,128)(2,1)} %get-tuple-element.161), channel_id=1, source_target_pairs={{0,64},{8,72},{16,80},{24,88},{32,96},{40,104},{48,112},{56,120},{... | collective-permute-start | bytes 1572872 | tf_op jit(solution)/shard_map/cond/branch_8_fun/ppermute | solution.py:28
  12.2 1.6 %fetch.18.w_ref = bf16[1024,1024]{1,0:T(8,128)(2,1)S(1)} custom-call(bf16[1024,4096]{1,0:T(8,128)(2,1)} %get-tuple-element.162.w_uvqk_ref), custom_call_target="tpu_custom_call" | custom-call | tf_op jit(solution)/shard_map/cond/branch_8_fun/fetch/pallas_call | solution.py:167
  13.8 23.6 %collective-permute-done.15.tokens_ref = bf16[256,1024]{1,0:T(8,128)(2,1)S(1)} collective-permute-done((bf16[256,1024]{1,0:T(8,128)(2,1)}, bf16[256,1024]{1,0:T(8,128)(2,1)S(1)}, u32[]{:S(2)}, u32[]{:S(2)}) %collective-permute-start.15) | collective-permute-done | bytes 524320 | tf_op jit(solution)/shard_map/cond/branch_8_fun/ppermute | solution.py:28
  37.5 1.6 %project_query.18 = (bf16[256,1024]{1,0:T(8,128)(2,1)}, bf16[8,256,128]{2,1,0:T(8,128)(2,1)}) custom-call(bf16[256,1024]{1,0:T(8,128)(2,1)S(1)} %collective-permute-done.15.tokens_ref, bf16[1024,1024]{1,0:T(8,128)(2,1)S(1)} %fetch.18.w_ref), custom_call_target="tpu_custom_call" | custom-call | flops 536870912 | bytes 2097152 | tf_op jit(solution)/shard_map/cond/branch_8_fun/project_query/pallas_call | solution.py:206
  39.1 0.0 all-to-all-done.8
  39.1 5.4 %all-to-all-start.10 = ((bf16[8,256,128]{2,1,0:T(8,128)(2,1)}), bf16[8,256,128]{2,1,0:T(8,128)(2,1)S(1)}, u32[]{:S(2)}, u32[]{:S(2)}) async-start(bf16[8,256,128]{2,1,0:T(8,128)(2,1)} %get-tuple-element.182.query_ref), calls=%async_computation.10 | async-start | bytes 1048576 | tf_op jit(solution)/shard_map/all_to_all | solution.py:21
  44.5 0.1 pad.2.clone
  44.6 0.0 copy-done.4
  44.6 0.0 copy-done.5
  44.6 0.2 fusion.meta_ref.facts_ref
  44.8 2.0 %visible_prefix.1 = (bf16[8,384,128]{2,1,0:T(8,128)(2,1)S(1)}, bf16[8,384,128]{2,1,0:T(8,128)(2,1)S(1)}) custom-call(s32[3]{0:T(128)S(1)} %fusion.meta_ref.facts_ref, bf16[8,2,384,128]{3,2,1,0:T(8,128)(2,1)} %get-tuple-element.183.cache_ref), custom_call_target="tpu_custom_call" | custom-call | tf_op jit(solution)/shard_map/visible_prefix/pallas_call | solution.py:309
  46.8 7.6 %all-to-all-done.10.query_ref = bf16[8,256,128]{2,1,0:T(8,128)(2,1)S(1)} async-done(((bf16[8,256,128]{2,1,0:T(8,128)(2,1)}), bf16[8,256,128]{2,1,0:T(8,128)(2,1)S(1)}, u32[]{:S(2)}, u32[]{:S(2)}) %all-to-all-start.10) | async-done | bytes 524320 | tf_op jit(solution)/shard_map/all_to_all | solution.py:21
  54.4 0.0 copy-start.3
  54.4 7.7 %attend.1 = bf16[8,256,128]{2,1,0:T(8,128)(2,1)} custom-call(bf16[8,256,128]{2,1,0:T(8,128)(2,1)S(1)} %all-to-all-done.10.query_ref, bf16[8,384,128]{2,1,0:T(8,128)(2,1)S(1)} %get-tuple-element.184.keys_ref, bf16[8,384,128]{2,1,0:T(8,128)(2,1)S(1)} %get-tuple-element.185.values_ref), custom_call_target="tpu_custom_call" | custom-call | flops 3221225472 | bytes 1572864 | tf_op jit(solution)/shard_map/attend/pallas_call | solution.py:351
  62.1 3.5 %all-to-all-start.11 = ((bf16[8,256,128]{2,1,0:T(8,128)(2,1)}), bf16[8,256,128]{2,1,0:T(8,128)(2,1)S(1)}, u32[]{:S(2)}, u32[]{:S(2)}) async-start(bf16[8,256,128]{2,1,0:T(8,128)(2,1)} %attend.1), calls=%async_computation.11 | async-start | bytes 1048576 | tf_op jit(solution)/shard_map/all_to_all | solution.py:21
  65.6 0.0 copy-done.3
  65.6 0.0 copy-start
  65.6 5.6 %project_own.1 = (bf16[256,1024]{1,0:T(8,128)(2,1)S(1)}, bf16[8,256,128]{2,1,0:T(8,128)(2,1)S(1)}) custom-call(bf16[256,1024]{1,0:T(8,128)(2,1)} %get-tuple-element.186.tokens_ref, bf16[8,256,128]{2,1,0:T(8,128)(2,1)} %get-tuple-element.182.query_ref, f32[1,1024]{1,0:T(1,128)S(1)} %bitcast.9, bf16[1024,4096]{1,0:T(8,128)(2,1)} %w_ref.2), custom_call_target="tpu_custom_call" | custom-call | flops 1610612736 | bytes 6291456 | tf_op jit(solution)/shard_map/project_own/pallas_call | solution.py:267
  71.2 0.0 copy-start.1
  71.2 0.8 copy-done.1
  72.0 3.7 %all-to-all-done.11.mixed_ref = bf16[8,256,128]{2,1,0:T(8,128)(2,1)S(1)} async-done(((bf16[8,256,128]{2,1,0:T(8,128)(2,1)}), bf16[8,256,128]{2,1,0:T(8,128)(2,1)S(1)}, u32[]{:S(2)}, u32[]{:S(2)}) %all-to-all-start.11) | async-done | bytes 524320 | tf_op jit(solution)/shard_map/all_to_all | solution.py:21
  75.8 0.0 copy-done
  75.8 0.0 copy-start.2
  75.8 1.0 %copy-done.2 = bf16[8,256,128]{2,1,0:T(8,128)(2,1)S(1)} copy-done((bf16[8,256,128]{2,1,0:T(8,128)(2,1)S(1)}, bf16[8,256,128]{2,1,0:T(8,128)(2,1)}, u32[]{:S(2)}) %copy-start.2) | copy-done | bytes 524312
  76.8 2.1 %finish.1 = bf16[256,1024]{1,0:T(8,128)(2,1)} custom-call(s32[3]{0:T(128)S(1)} %fusion.meta_ref.facts_ref, bf16[8,256,128]{2,1,0:T(8,128)(2,1)S(1)} %all-to-all-done.11.mixed_ref, bf16[8,256,128]{2,1,0:T(8,128)(2,1)S(1)} %copy-done.2, bf16[256,1024]{1,0:T(8,128)(2,1)S(1)} %get-tuple-element.188.gate_ref, bf16[1024,1024]{1,0:T(8,128)(2,1)S(1)} %copy-done), custom_call_target="tpu_custom_call" | custom-call | flops 536870912 | bytes 2097152 | tf_op jit(solution)/shard_map/finish/pallas_call | solution.py:400
  (1 shorter events, 0.0 us)
Async XLA Ops:
  3.4 41.2 %copy-start.4 = (s32[32]{0:T(128)S(1)}, s32[32]{0:T(128)}, u32[]{:S(2)}) copy-start(s32[32]{0:T(128)} %param.34) | copy-start | bytes 388
  3.4 41.2 %copy-start.5 = (s32[32]{0:T(128)S(1)}, s32[32]{0:T(128)}, u32[]{:S(2)}) copy-start(s32[32]{0:T(128)} %param.33) | copy-start | bytes 388
  3.6 35.5 %all-to-all-start.8 = ((bf16[8,2,384,128]{3,2,1,0:T(8,128)(2,1)}), bf16[8,2,384,128]{3,2,1,0:T(8,128)(2,1)}, u32[]{:S(2)}, u32[]{:S(2)}) async-start(bf16[8,2,384,128]{3,2,1,0:T(8,128)(2,1)} %get-tuple-element.164), calls=%async_computation.8 | async-start | bytes 3145728 | tf_op jit(solution)/shard_map/cond/branch_8_fun/all_to_all | solution.py:21
  9.0 28.5 %collective-permute-start.15 = (bf16[256,1024]{1,0:T(8,128)(2,1)}, bf16[256,1024]{1,0:T(8,128)(2,1)S(1)}, u32[]{:S(2)}, u32[]{:S(2)}) collective-permute-start(bf16[256,1024]{1,0:T(8,128)(2,1)} %get-tuple-element.161), channel_id=1, source_target_pairs={{0,64},{8,72},{16,80},{24,88},{32,96},{40,104},{48,112},{56,120},{... | collective-permute-start | bytes 1572872 | tf_op jit(solution)/shard_map/cond/branch_8_fun/ppermute | solution.py:28
  39.1 15.3 %all-to-all-start.10 = ((bf16[8,256,128]{2,1,0:T(8,128)(2,1)}), bf16[8,256,128]{2,1,0:T(8,128)(2,1)S(1)}, u32[]{:S(2)}, u32[]{:S(2)}) async-start(bf16[8,256,128]{2,1,0:T(8,128)(2,1)} %get-tuple-element.182.query_ref), calls=%async_computation.10 | async-start | bytes 1048576 | tf_op jit(solution)/shard_map/all_to_all | solution.py:21
  54.4 11.2 %copy-start.3 = (f32[1024]{0:T(1024)S(1)}, f32[1024]{0:T(1024)}, u32[]{:S(2)}) copy-start(f32[1024]{0:T(1024)} %param.31) | copy-start | bytes 12292
  62.1 13.7 %all-to-all-start.11 = ((bf16[8,256,128]{2,1,0:T(8,128)(2,1)}), bf16[8,256,128]{2,1,0:T(8,128)(2,1)S(1)}, u32[]{:S(2)}, u32[]{:S(2)}) async-start(bf16[8,256,128]{2,1,0:T(8,128)(2,1)} %attend.1), calls=%async_computation.11 | async-start | bytes 1048576 | tf_op jit(solution)/shard_map/all_to_all | solution.py:21
  65.6 10.2 %copy-start = (bf16[1024,1024]{1,0:T(8,128)(2,1)S(1)}, bf16[1024,1024]{1,0:T(8,128)(2,1)}, u32[]{:S(2)}) copy-start(bf16[1024,1024]{1,0:T(8,128)(2,1)} %w_ref.3) | copy-start | bytes 6291460
  71.2 0.8 %copy-start.1 = (bf16[8,256,128]{2,1,0:T(8,128)(2,1)}, bf16[8,256,128]{2,1,0:T(8,128)(2,1)S(1)}, u32[]{:S(2)}) copy-start(bf16[8,256,128]{2,1,0:T(8,128)(2,1)S(1)} %get-tuple-element.187.own_ref) | copy-start | bytes 1572868
  75.8 1.0 %copy-start.2 = (bf16[8,256,128]{2,1,0:T(8,128)(2,1)S(1)}, bf16[8,256,128]{2,1,0:T(8,128)(2,1)}, u32[]{:S(2)}) copy-start(bf16[8,256,128]{2,1,0:T(8,128)(2,1)} %copy-done.1) | copy-start | bytes 1572868
